TPU v7x, 128 devices: a whole 4x4x4 slice. The times are simulated.
128 devices in a mesh: dp: 8 (over x, core), fsdp: 8 (over z_lo, y), mp: 2 (over z_hi).
Axes of the slice: x: 4, y: 4, z: 4 (z_hi: 2, z_lo: 2; z = z_hi * 2 + z_lo), core: 2. Of those that a mesh axis runs over, the one named last changes fastest.
Arguments:
- tokens_in: bfloat16 [16384, 3072], P(('dp', 'fsdp', 'mp')), may hold values from -40 to 40
- segment_ids: int32 [16384], P(('dp', 'fsdp', 'mp')), may hold values from 0 to 63, never falling along the last dimension, each value on 1 to 1024 neighbouring positions
- target_ids: int32 [16384], P(('dp', 'fsdp', 'mp')), may hold values from 0 to 16383
- old_weights: bfloat16 [4, 3072, 4096], P(None, ('dp', 'fsdp', 'mp'))
- old_first: float32 [4, 3072, 4096], P(None, ('dp', 'fsdp', 'mp')), may hold values from -6 to 6
- old_second: float32 [4, 3072, 4096], P(None, ('dp', 'fsdp', 'mp')), may hold values from 0.01 to 4
- old_block: int32 [128], P(('dp', 'fsdp', 'mp')), may hold values from 0 to 127, each once
- new_residue: int32 [8], P('dp'), may hold values from 0 to 7, each once
- norm_gain: float32 [3072], replicated, may hold values from 0.5 to 1.5
- head_weight: bfloat16 [3072, 16384], P(None, ('fsdp', 'mp'))
Outputs:
- new_weights: bfloat16 [4, 3072, 4096], P(None, 'dp', ('fsdp', 'mp'))
- new_first: float32 [4, 3072, 4096], P(None, 'dp', ('fsdp', 'mp'))
- new_second: float32 [4, 3072, 4096], P(None, 'dp', ('fsdp', 'mp'))
- loss: float32 [16384], P(('dp', 'fsdp', 'mp'))
Inputs may be any that keep to these rules, and one draw needn't show every extreme that they name: `old_block`: a permutation of the old layout's row blocks. `new_residue`: a permutation; index i of dp holds the rows whose number modulo 8 is new_residue[i], in rising order. `segment_ids`: never falling along the tokens.
All inputs are finite; a program needn't handle non-finite values.
Results may differ from a plain program's by a relative error of at most 0.0075.
Values may be sent and summed in bfloat16 or wider, within the bound.
A program may use at most 192 MiB of HBM per device.

v0:
```python
import math

import jax
import jax.numpy as jnp
from jax import lax
from jax.sharding import PartitionSpec as P

HD = 128


def copy_for_each(value, axis):
    copies = jnp.broadcast_to(value, (lax.axis_size(axis), *value.shape))
    return lax.all_to_all(copies, axis, split_axis=0, concat_axis=0, tiled=True)


def laid_out(tiles, dim):
    tiles = jnp.moveaxis(tiles, 0, dim)
    dims = tiles.shape
    return tiles.reshape(*dims[:dim], dims[dim] * dims[dim + 1], *dims[dim + 2 :])


def gathered_copies(value, axis, dim):
    tiles = copy_for_each(value, axis)
    return laid_out(tiles, dim)


def side_by_side(arrays, axis, split_dim, concat_dim, along):
    ends, at = ([], 0)
    for a in arrays[:-1]:
        at += a.shape[along]
        ends.append(at)
    both = jnp.concatenate(arrays, axis=along)
    return tuple(
        jnp.split(
            lax.all_to_all(both, axis, split_axis=split_dim, concat_axis=concat_dim, tiled=True),
            ends,
            axis=along,
        )
    )


def turned_gather(arrays, axis, dims):
    turned = [jnp.moveaxis(a, dim, 0) for a, dim in zip(arrays, dims)]
    widths = [t[0].size for t in turned]
    both = jnp.concatenate([t.reshape(-1, w) for t, w in zip(turned, widths)], axis=1)
    result = lax.all_gather(both, axis, axis=0, tiled=True)
    tiles = jnp.split(result, [sum(widths[:k]) for k in range(1, len(widths))], axis=1)
    return tuple(
        (
            jnp.moveaxis(b.reshape(-1, *t.shape[1:]), 0, dim)
            for b, t, dim in zip(tiles, turned, dims)
        )
    )


def gathered_once(value, axis):
    leaves = jax.tree.leaves(value)
    sequence = sorted(range(len(leaves)), key=lambda k: -leaves[k].size)
    width = (1, *leaves[sequence[0]].shape)[-1]
    lines = [
        jnp.pad(leaves[k].reshape(-1), (0, -leaves[k].size % width)).reshape(-1, width)
        for k in sequence
    ]
    both, at, found = (copy_for_each(jnp.concatenate(lines), axis), 0, {})
    for k, line in zip(sequence, lines):
        piece = both[:, at : at + len(line)].reshape(len(both), -1)
        found[k] = piece[:, : leaves[k].size].reshape(-1, *leaves[k].shape)
        at += len(line)
    numbers = iter(range(len(leaves)))
    return jax.tree.map(lambda _: found[next(numbers)], value)


def joined_by_halves(pieces, combine):
    while len(jax.tree.leaves(pieces)[0]) > 1:
        pieces = jax.vmap(combine)(
            *(jax.tree.map(lambda part: part[side::2], pieces) for side in (0, 1))
        )
    return jax.tree.map(lambda part: part[0], pieces)


def joined_all(value, axis, combine):
    pieces = gathered_once(value, axis)
    return joined_by_halves(pieces, combine)


def inverse_of(table):
    total_count = table.shape[0]
    places = jnp.arange(total_count, dtype=jnp.int32)
    return jnp.sum(jnp.where(table[None, :] == places[:, None], places[None, :], 0), axis=1)


def pack_rows(stored, residues, fm_count):
    matrices, row_count, columns = stored.shape
    dp_count = residues.shape[0]
    split_rows = stored.reshape(
        matrices, row_count // dp_count, dp_count, fm_count, columns // fm_count
    )
    chosen = jnp.take(split_rows, residues, axis=2)
    return chosen.transpose(2, 3, 0, 1, 4).reshape(
        dp_count * fm_count, matrices, row_count // dp_count, columns // fm_count
    )


def unpack_rows(received, holder):
    ordered = jnp.take(received, holder, axis=0)
    devices, matrices, pair_rows, group_cols = ordered.shape
    return ordered.transpose(1, 0, 2, 3).reshape(matrices, devices * pair_rows, group_cols)


def norm_rows(hidden, norm_gain):
    scale = lax.rsqrt(jnp.mean(hidden * hidden, axis=1, keepdims=True) + 1e-05)
    return (hidden * scale * norm_gain).astype(jnp.bfloat16)


def combine_parts(earlier, later):
    joint_max = jnp.maximum(earlier[0], later[0])
    joint_total = earlier[1] * jnp.exp(earlier[0] - joint_max) + later[1] * jnp.exp(
        later[0] - joint_max
    )
    return (joint_max, joint_total, earlier[2] + later[2])


def body(
    tokens_in,
    segment_ids,
    target_ids,
    old_weights,
    old_first,
    old_second,
    old_block,
    new_residue,
    norm_gain,
    head_weight,
):
    dp_count = lax.axis_size("dp")
    fm_count = lax.axis_size(("fsdp", "mp"))
    matrices, old_rows, columns = old_weights.shape
    group_cols = columns // fm_count
    table_all = lax.all_gather(old_block, ("dp", "fsdp", "mp"), axis=0, tiled=True)
    residues = gathered_copies(new_residue, "dp", 0)
    holder = inverse_of(table_all)
    first_sent = pack_rows(old_first, residues, fm_count)
    second_sent = pack_rows(old_second, residues, fm_count)
    first_got, second_got = side_by_side((first_sent, second_sent), ("dp", "fsdp", "mp"), 0, 0, 1)
    new_first = unpack_rows(first_got, holder)
    new_second = unpack_rows(second_got, holder)
    whole_tokens = lax.all_gather(tokens_in, ("fsdp", "mp"), axis=0, tiled=True)
    segments, targets = turned_gather((segment_ids, target_ids), ("fsdp", "mp"), (0, 0))
    seq_len, model_width = whole_tokens.shape
    new_rows = model_width // dp_count
    by_group = old_weights.reshape(matrices, old_rows, fm_count, group_cols).transpose(2, 0, 1, 3)
    spread = jnp.broadcast_to(by_group[None], (dp_count,) + by_group.shape)
    spread = spread.reshape(dp_count * fm_count, matrices, old_rows, group_cols)
    weights_got = lax.all_to_all(
        spread, ("dp", "fsdp", "mp"), split_axis=0, concat_axis=0, tiled=True
    )
    logical = (
        jnp.take(weights_got, holder, axis=0)
        .transpose(1, 0, 2, 3)
        .reshape(matrices, model_width, group_cols)
    )
    new_weights = lax.dynamic_index_in_dim(
        logical.reshape(matrices, new_rows, dp_count, group_cols), new_residue[0], 2, keepdims=False
    )
    projected = jnp.einsum(
        "sd,mdc->msc", whole_tokens, logical[:3], preferred_element_type=jnp.float32
    )
    heads = group_cols // HD
    queries = projected[0].astype(jnp.bfloat16).reshape(seq_len, heads, HD)
    keys_all = projected[1].astype(jnp.bfloat16).reshape(seq_len, heads, HD)
    values_all = projected[2].astype(jnp.bfloat16).reshape(seq_len, heads, HD)
    positions_all = jnp.arange(seq_len, dtype=jnp.int32)
    allowed = (positions_all[:, None] >= positions_all[None, :]) & (
        segments[:, None] == segments[None, :]
    )
    scores = jnp.einsum("shd,thd->hst", queries, keys_all, preferred_element_type=jnp.float32) * (
        1.0 / math.sqrt(HD)
    )
    scores = jnp.where(allowed[None], scores, -1e30)
    row_max = jnp.max(scores, axis=2, keepdims=True)
    expo = jnp.where(allowed[None], jnp.exp(scores - row_max), 0.0)
    soft = (expo / jnp.sum(expo, axis=2, keepdims=True)).astype(jnp.bfloat16)
    attended = jnp.einsum("hst,thd->shd", soft, values_all, preferred_element_type=jnp.float32)
    attended = attended.astype(jnp.bfloat16).reshape(seq_len, group_cols)
    partial_value = jnp.einsum(
        "sc,dc->sd", attended, logical[3], preferred_element_type=jnp.float32
    )
    summed = lax.psum(partial_value.astype(jnp.bfloat16), ("fsdp", "mp")).astype(jnp.float32)
    normed = norm_rows(whole_tokens.astype(jnp.float32) + summed, norm_gain)
    logits = jnp.dot(normed, head_weight, preferred_element_type=jnp.float32)
    vocab_dev = logits.shape[1]
    offset = lax.axis_index(("fsdp", "mp")) * vocab_dev
    row_top = jnp.max(logits, axis=1)
    row_total = jnp.sum(jnp.exp(logits - row_top[:, None]), axis=1)
    vocab_ids = jnp.arange(vocab_dev, dtype=jnp.int32) + offset
    picked = jnp.sum(jnp.where(vocab_ids[None, :] == targets[:, None], logits, 0.0), axis=1)
    joint_max, joint_total, joint_picked = joined_all(
        (row_top, row_total, picked), ("fsdp", "mp"), combine_parts
    )
    token_loss = joint_max + jnp.log(joint_total) - joint_picked
    own_count = tokens_in.shape[0]
    own_start = lax.axis_index(("fsdp", "mp")) * own_count
    loss = lax.dynamic_slice_in_dim(token_loss, own_start, own_count)
    return (new_weights, new_first, new_second, loss)


def solution(mesh):
    placed = (
        P(("dp", "fsdp", "mp"), None),
        P(("dp", "fsdp", "mp")),
        P(("dp", "fsdp", "mp")),
        P(None, ("dp", "fsdp", "mp"), None),
        P(None, ("dp", "fsdp", "mp"), None),
        P(None, ("dp", "fsdp", "mp"), None),
        P(("dp", "fsdp", "mp")),
        P("dp"),
        P(),
        P(None, ("fsdp", "mp")),
    )
    return jax.shard_map(
        body,
        mesh=mesh,
        in_specs=placed,
        out_specs=(
            P(None, "dp", ("fsdp", "mp")),
            P(None, "dp", ("fsdp", "mp")),
            P(None, "dp", ("fsdp", "mp")),
            P(("dp", "fsdp", "mp")),
        ),
        check_vma=False,
    )
```

profile of v0, /device:TPU:1, one launch (start us, length us, event | category | flops | bytes accessed | tf_op | source)
XLA Modules:
  0.0 789.4 jit_solution(8790189344194897286)
XLA Ops:
  7.2 0.7 all-gather.2.cloned.1.call-update
  7.9 1.3 copy.98
  9.5 3.4 broadcast_in_dim.90
  13.0 11.9 %all-to-all-start = ((bf16[128,4,24,256]{3,2,1,0:T(8,128)(2,1)}), bf16[128,4,24,256]{3,2,1,0:T(8,128)(2,1)}, u32[]{:S(2)}, u32[]{:S(2)}) async-start(bf16[128,4,24,256]{3,2,1,0:T(8,128)(2,1)} %bitcast.93), calls=%async_computation | async-start | bytes 12582912 | tf_op jit(solution)/shard_map/all_to_all | solution.py:154
  25.7 377.7 %all-reduce = s32[128]{0:T(128)S(1)} all-reduce(s32[128]{0:T(128)S(1)} %dynamic-update-slice), channel_id=1, replica_groups=mesh['dp'=8,'fsdp'=8,'mp'=2] {'dp','fsdp','mp'}, use_global_device_ids=true, to_apply=%add | all-reduce | flops 128 | bytes 1024
  403.4 30.0 %all_gather.11 = s32[2048,2]{0,1:T(2,128)S(1)} all-gather(s32[128,2]{0,1:T(2,128)S(1)} %pad_add_fusion), channel_id=1, replica_groups=mesh['dp'=8,'fsdp'=8,'mp'=2] {'fsdp','mp'}, dimensions={0}, use_global_device_ids=true | all-gather | bytes 17408 | tf_op jit(solution)/shard_map/all_gather | solution.py:46
  433.5 0.6 fusion.38
  434.1 5.3 fusion.4
  439.5 6.4 gather_fusion
  445.9 3.4 select_bitcast_fusion
  449.6 2.2 copy-done
  451.9 2.4 copy.81
  454.3 14.3 %fusion.17 = bf16[3,2048,256]{1,2,0:T(8,128)(2,1)S(1)} fusion(bf16[3,3072,256]{2,1,0:T(8,128)(2,1)} %bitcast.101, bf16[2048,3072]{1,0:T(8,128)(2,1)} %all-gather.2.cloned.1.call-done), kind=kOutput, calls=%fused_computation.31 | convolution fusion | flops 9665249280 | bytes 20447232 | tf_op jit(solution)/shard_map/sd,mdc->msc/dot_general | solution.py:165
  468.7 1.2 fusion.33
  469.9 23.0 %fusion.39 = (f32[2,2048]{1,0:T(2,128)S(1)}, f32[2,2048,2048]{1,2,0:T(8,128)}) fusion(pred[2048,2048]{0,1:T(8,128)(4,1)} %fusion.4, bf16[2048,2,128]{0,2,1:T(8,128)(2,1)} %bitcast.108, bf16[2048,2,128]{0,2,1:T(8,128)(2,1)S(1)} %bitcast.107), kind=kOutput, calls=%fused_computation.88 | convolution fusion | flops 2189428736 | bytes 39862272 | tf_op jit(solution)/shard_map/sub | solution.py:181
  492.9 12.1 %fusion.20 = bf16[2,128,2048]{2,1,0:T(8,128)(2,1)S(1)} fusion(bf16[2048,2,128]{0,2,1:T(8,128)(2,1)S(1)} %bitcast.106, f32[2,2048,2048]{1,2,0:T(8,128)} %get-tuple-element.55, f32[2,2048]{1,0:T(2,128)S(1)} %get-tuple-element.54), kind=kOutput, calls=%fused_computation.32 | convolution fusion | flops 2164785152 | bytes 35667968 | tf_op jit(solution)/shard_map/hst,thd->shd/dot_general | solution.py:183
  505.0 6.5 convolution_convert_fusion
  512.3 0.6 broadcast_in_dim.92
  512.9 11.1 %all-to-all-start.1 = ((s32[8,1,1]{2,1,0:T(1,128)}), s32[8,1,1]{2,1,0:T(1,128)S(1)}, u32[]{:S(2)}, u32[]{:S(2)}) async-start(s32[8,1,1]{2,1,0:T(1,128)} %broadcast_in_dim.92), calls=%async_computation.1 | async-start | bytes 8192 | tf_op jit(solution)/shard_map/all_to_all | solution.py:13
  524.0 0.5 copy.99
  524.5 2.0 copy.100
  526.4 2.2 all-to-all-done.1
  528.9 1.8 gather_fusion.1
  530.7 0.6 gather_fusion.2
  531.3 1.9 select_bitcast_fusion.2
  533.4 1.0 copy.79
  534.5 1.0 copy.80
  535.5 2.3 pad_maximum_fusion
  537.9 4.3 all-to-all-start.2
  542.3 47.7 %all-to-all-done.2 = f32[128,8,3,256]{3,1,2,0:T(8,128)S(1)} async-done(((f32[128,8,3,256]{3,1,2,0:T(8,128)}), f32[128,8,3,256]{3,1,2,0:T(8,128)S(1)}, u32[]{:S(2)}, u32[]{:S(2)}) %all-to-all-start.2) | async-done | bytes 3145760 | tf_op jit(solution)/shard_map/all_to_all | solution.py:35
  590.0 2.1 fusion.34
  592.1 4.0 gather_fusion.4
  596.1 3.9 gather_fusion.3
  600.0 127.2 %all-reduce.3.cloned.1.call-done = bf16[2048,3072]{1,0:T(8,128)(2,1)} async-done(((bf16[2048,3072]{1,0:T(8,128)(2,1)}), bf16[2048,3072]{1,0:T(8,128)(2,1)}) %all-reduce.3.cloned.1.call-update) | async-done | bytes 12582928 | tf_op jit(solution)/shard_map/psum | solution.py:188
  727.2 11.0 %multiply_reduce_fusion = f32[2048]{0:T(1024)S(1)} fusion(bf16[2048,3072]{1,0:T(8,128)(2,1)} %all-reduce.3.cloned.1.call-done, bf16[2048,3072]{1,0:T(8,128)(2,1)} %all-gather.2.cloned.1.call-done), kind=kLoop, calls=%fused_computation.11 | loop fusion | flops 31455232 | bytes 25174016 | tf_op jit(solution)/shard_map/reduce_sum | solution.py:111
  738.2 1.0 copy-done.1
  739.2 20.2 %fusion.40 = (f32[2048]{0:T(1024)S(1)}, f32[2048,1024]{0,1:T(8,128)}) fusion(bf16[3072,1024]{1,0:T(8,128)(2,1)} %param.23, bf16[2048,3072]{1,0:T(8,128)(2,1)S(1)} %copy-done.1, bf16[2048,3072]{1,0:T(8,128)(2,1)} %all-gather.2.cloned.1.call-done, f32[3072]{0:T(1024)S(1)} %copy-done.8, f32[2048]{0:T(1024)S(1)} %add_rsqrt_fusion), kind=kOutput, calls=%fused_computation.89 | convolution fusion | flops 12924745728 | bytes 39874560 | tf_op jit(solution)/shard_map/dot_general | solution.py:190
  759.4 4.6 exponential_reduce_fusion
  764.0 0.9 broadcast_in_dim.97
  765.0 5.5 all-to-all-start.3
  770.5 2.8 broadcast_select_fusion
  773.3 1.4 copy.89
  774.7 1.4 copy.88
  776.1 0.4 copy.76
  776.5 1.6 constant_dynamic-slice_fusion.6
  778.2 1.0 copy.105
  779.2 1.1 all-to-all-done.3
  781.6 0.5 fusion.30
  (80 shorter events, 2.7 us)
Async XLA Ops:
  7.2 447.1 %all-gather.2.cloned.1.call-start = ((), (), s32[]{:S(2)}) async-start(), calls=%async_computation.4 | async-start | bytes 13369344 | tf_op jit(solution)/shard_map/all_gather | solution.py:147
  13.0 390.4 %copy-start.6 = (s32[128]{0:T(128)S(1)}, s32[128]{0:T(128)}, u32[]{:S(2)}) copy-start(s32[128]{0:T(128)} %param.16) | copy-start | bytes 1540
  13.0 390.4 %copy-start.7 = (s32[128]{0:T(128)S(1)}, s32[128]{0:T(128)}, u32[]{:S(2)}) copy-start(s32[128]{0:T(128)} %param.15) | copy-start | bytes 1540
  13.0 426.5 %all-to-all-start = ((bf16[128,4,24,256]{3,2,1,0:T(8,128)(2,1)}), bf16[128,4,24,256]{3,2,1,0:T(8,128)(2,1)}, u32[]{:S(2)}, u32[]{:S(2)}) async-start(bf16[128,4,24,256]{3,2,1,0:T(8,128)(2,1)} %bitcast.93), calls=%async_computation | async-start | bytes 12582912 | tf_op jit(solution)/shard_map/all_to_all | solution.py:154
  24.9 702.4 %all-reduce.3.cloned.1.call-start = ((), (), s32[]{:S(2)}) async-start(), calls=%async_computation.5 | async-start | bytes 25165824 | tf_op jit(solution)/shard_map/psum | solution.py:188
  433.5 12.4 %copy-start.4 = (pred[128]{0:T(512)(128)(4,1)}, pred[128]{0:T(512)(128)(4,1)S(1)}, u32[]{:S(2)}) copy-start(pred[128]{0:T(512)(128)(4,1)S(1)} %compare_and_fusion.1) | copy-start | bytes 388
  449.3 2.6 copy-start
  492.9 12.2 %slice-start.2 = ((bf16[4,128,24,256]{3,2,0,1:T(8,128)(2,1)}), bf16[1,128,24,256]{3,2,0,1:T(8,128)(2,1)S(1)}, s32[]{:S(2)}) async-start(bf16[4,128,24,256]{3,2,0,1:T(8,128)(2,1)} %copy-done), calls=%async_computation.8 | async-start | bytes 3145728 | tf_op jit(solution)/shard_map/slice | solution.py:186
  511.5 12.5 %copy-start.2 = (f32[4,24,4096]{2,1,0:T(8,128)S(1)}, f32[4,24,4096]{2,1,0:T(8,128)}, u32[]{:S(2)}) copy-start(f32[4,24,4096]{2,1,0:T(8,128)} %param.18) | copy-start | bytes 4718596
  512.9 15.7 %all-to-all-start.1 = ((s32[8,1,1]{2,1,0:T(1,128)}), s32[8,1,1]{2,1,0:T(1,128)S(1)}, u32[]{:S(2)}, u32[]{:S(2)}) async-start(s32[8,1,1]{2,1,0:T(1,128)} %broadcast_in_dim.92), calls=%async_computation.1 | async-start | bytes 8192 | tf_op jit(solution)/shard_map/all_to_all | solution.py:13
  537.9 52.1 %all-to-all-start.2 = ((f32[128,8,3,256]{3,1,2,0:T(8,128)}), f32[128,8,3,256]{3,1,2,0:T(8,128)S(1)}, u32[]{:S(2)}, u32[]{:S(2)}) async-start(f32[128,8,3,256]{3,1,2,0:T(8,128)} %pad_maximum_fusion), calls=%async_computation.2 | async-start | bytes 6291456 | tf_op jit(solution)/shard_map/all_to_all | solution.py:35
  600.0 138.2 %copy-start.8 = (f32[3072]{0:T(1024)S(1)}, f32[3072]{0:T(1024)}, u32[]{:S(2)}) copy-start(f32[3072]{0:T(1024)} %param.22) | copy-start | bytes 36868
  727.2 12.0 %copy-start.1 = (bf16[2048,3072]{1,0:T(8,128)(2,1)S(1)}, bf16[2048,3072]{1,0:T(8,128)(2,1)}, u32[]{:S(2)}) copy-start(bf16[2048,3072]{1,0:T(8,128)(2,1)} %all-reduce.3.cloned.1.call-done) | copy-start | bytes 37748740
  739.2 20.2 %copy-start.3 = (s32[2048,1]{0,1:T(1,128)S(1)}, s32[2048,1]{0,1:T(1,128)}, u32[]{:S(2)}) copy-start(s32[2048,1]{0,1:T(1,128)} %get-tuple-element.48) | copy-start | bytes 24580
  759.4 11.1 %copy-start.5 = (pred[128]{0:T(512)(128)(4,1)S(1)}, pred[128]{0:T(512)(128)(4,1)}, u32[]{:S(2)}) copy-start(pred[128]{0:T(512)(128)(4,1)} %copy-done.4) | copy-start | bytes 388
  765.0 11.2 %slice-start = ((s8[6291456]{0:T(1024)(128)(4,1)}), s8[2097152]{0:T(1024)(128)(4,1)S(1)}, s32[]{:S(2)}) async-start(s8[6291456]{0:T(1024)(128)(4,1)} %bitcast.90), calls=%async_computation.6 | async-start | bytes 4194304
  765.0 15.4 %all-to-all-start.3 = ((f32[16,3,2048]{2,1,0:T(4,128)}), f32[16,3,2048]{2,1,0:T(4,128)S(1)}, u32[]{:S(2)}, u32[]{:S(2)}) async-start(f32[16,3,2048]{2,1,0:T(4,128)} %broadcast_in_dim.97), calls=%async_computation.3 | async-start | bytes 1048576 | tf_op jit(solution)/shard_map/all_to_all | solution.py:13
  770.5 5.7 slice-start.1
Sparse Core Ops, SparseCore 0:
  9.6 335.1 all-gather.1
  511.7 215.4 all-reduce.2
where the time goes:
time: 799 us; the launch traced here: 789 us
  blocking collectives  408 us (51%)
  waiting for transfers between devices  179 us (22%)
  matrix products  76.2 us (10%)
  local copies, waits for them, and re-layouts  45 us (6%)
  starting transfers between devices  32.9 us (4%)
  other arithmetic  32.5 us (4%)
  between operations  16.4 us (2%)
    unnamed x1, blocking collectives  378 us
    psum x1, waiting for transfers between devices, body(): lax.psum(partial_value.astype(jnp.bfloat16), ('fsdp', 'mp'))  127 us
    all_to_all x1, waiting for transfers between devices, side_by_side(): lax.all_to_all(both, axis, split_axis=split_dim, concat_axis=concat_dim,...  47.7 us
    all_gather x1, blocking collectives, turned_gather(): result = lax.all_gather(both, axis, axis=0, tiled=True)  30 us
    sub x1, matrix products, body(): expo = jnp.where(allowed[None], jnp.exp(scores - row_max), 0.0)  23 us
    dot_general x1, matrix products, body(): logits = jnp.dot(normed, head_weight, preferred_element_type=jnp.float32)  20.2 us
    all_to_all x2, starting transfers between devices, copy_for_each(): return lax.all_to_all(copies, axis, split_axis=0, concat_axis=0, tiled=True)  16.6 us
  transfers between devices with their start and end apart: 6, of which 4 were waited for; matrix products, arithmetic and copies ran while one was open for 7% of the time, Pallas kernels for 0%

commit v1 on v0

v1 whole, which is shorter than its diff:
```python
import functools
import math

import jax
import jax.numpy as jnp
from jax import lax
from jax.experimental import pallas as pl
from jax.experimental.pallas import tpu as pltpu
from jax.sharding import PartitionSpec as P

HD = 128
MESH = pl.DeviceIdType.MESH
A_END, A_MID, B_MID = 48, 32, 80
VMEM = pl.BlockSpec(memory_space=pltpu.VMEM)
ANY = pl.BlockSpec(memory_space=pl.ANY)


class Place:
    def __init__(self):
        self.dp = lax.axis_index("dp")
        self.fs = lax.axis_index("fsdp")
        self.g = lax.axis_index("mp")
        self.x, self.c = lax.div(self.dp, 2), lax.rem(self.dp, 2)
        self.zl, self.y = lax.div(self.fs, 4), lax.rem(self.fs, 4)
        self.fm = self.fs * 2 + self.g
        self.n = lax.rem(self.c + self.g, 2)

    def flip_z(self, rz):
        return 1 - self.zl if rz else self.zl

    def turn_y(self, ry):
        return lax.rem(self.y + ry, 4)

    def slot(self, rz, ry):
        z = self.flip_z(rz)
        return (z + self.n - 2 * z * self.n) * 8 + self.turn_y(ry) * 2 + self.c

    def other_slot(self, rz, ry):
        z, n = self.flip_z(rz), 1 - self.n
        return (z + n - 2 * z * n) * 8 + self.turn_y(ry) * 2 + 1 - self.c

    def at(self, rx=0, rz=0, ry=0):
        return (
            lax.rem(self.x + rx, 4) * 2 + self.c,
            self.flip_z(rz) * 4 + self.turn_y(ry),
            self.g,
        )

    def twin(self):
        return (self.x * 2 + 1 - self.c, self.fs, self.g)

    def across(self, core):
        return (self.x * 2 + core, (1 - self.zl) * 4 + self.y, 1 - self.g)


class Sends:
    def __init__(self, send_sem, recv_sem):
        self.send_sem, self.recv_sem, self.count, self.open = send_sem, recv_sem, 0, []

    def make(self, src, dst, device):
        k = self.count
        self.count += 1
        return pltpu.make_async_remote_copy(
            src_ref=src,
            dst_ref=dst,
            send_sem=self.send_sem.at[k],
            recv_sem=self.recv_sem.at[k],
            device_id=device,
            device_id_type=MESH,
        )

    def start(self, src, dst, device):
        copy = self.make(src, dst, device)
        copy.start()
        self.open.append(copy)
        return copy

    def finish(self):
        for copy in self.open:
            copy.wait_send()


def greet(devices):
    barrier = pltpu.get_barrier_semaphore()
    for device in devices:
        pl.semaphore_signal(barrier, inc=1, device_id=device, device_id_type=MESH)
    pl.semaphore_wait(barrier, len(devices))


class BlockGather:
    def __init__(self, me, full, sends):
        self.me, self.full, self.sends, self.got, self.twins = me, full, sends, {}, []

    def send(self, key, rz, ry, start, end, device):
        part = self.full.at[self.me.slot(rz, ry), pl.ds(start, end - start)]
        self.got[key] = self.sends.start(part, part, device)

    def wait(self, *keys):
        for key in keys:
            self.got[key].wait_recv()

    def share(self, rz, ry):
        block = self.full.at[self.me.slot(rz, ry)]
        self.twins.append(self.sends.start(block, block, self.me.twin()))

    def first(self):
        me = self.me
        self.up, self.down, self.over = me.at(ry=1), me.at(ry=3), me.at(rz=1)
        self.send("ay0", 0, 0, 0, A_END, self.up)
        self.send("ay1", 0, 0, 0, A_END, self.down)
        self.send("bz", 0, 0, A_END, 128, self.over)
        self.send("az0", 0, 0, 0, A_END, self.over)
        self.send("by0", 0, 0, A_END, 128, self.up)
        self.send("by1", 0, 0, A_END, 128, self.down)
        self.share(0, 0)

    def second(self):
        self.wait("ay0")
        self.send("af0", 0, 3, 0, A_MID, self.up)
        self.send("az3", 0, 3, 0, A_END, self.over)
        self.wait("ay1")
        self.send("af1", 0, 1, A_MID, A_END, self.down)
        self.send("az1", 0, 1, 0, A_END, self.over)
        self.wait("bz")
        self.send("by2", 1, 0, A_END, 128, self.up)
        self.send("by3", 1, 0, A_END, 128, self.down)

    def third(self):
        self.wait("af0", "af1")
        self.send("az2", 0, 2, 0, A_END, self.over)
        self.wait("by0")
        self.send("bf0", 0, 3, A_END, B_MID, self.up)
        self.wait("by1")
        self.send("bf1", 0, 1, B_MID, 128, self.down)
        self.share(0, 1)
        self.share(0, 3)
        self.wait("az0")
        self.share(1, 0)

    def fourth(self):
        self.wait("by2")
        self.send("bf2", 1, 3, A_END, B_MID, self.up)
        self.wait("by3")
        self.send("bf3", 1, 1, B_MID, 128, self.down)
        self.wait("az3", "az1")
        self.share(1, 1)
        self.share(1, 3)

    def last(self):
        self.wait("bf0", "bf1")
        self.share(0, 2)
        self.wait("az2", "bf2", "bf3")
        self.share(1, 2)
        for copy in self.twins:
            copy.wait_recv()


def gather_kernel(
    tok,
    small,
    wpk,
    xfull,
    sfull,
    wfull,
    wown,
    send_sem,
    recv_sem,
    local_sem,
    ex_send,
    ex_recv,
    small_send,
    small_recv,
):
    me = Place()
    sends = Sends(send_sem, recv_sem)
    mine = me.c * 16 + me.fm

    barrier = pltpu.get_barrier_semaphore()

    @pl.loop(1, 32)
    def _(k):
        q = lax.rem(mine + k, 32)
        fm = lax.rem(q, 16)
        device = (me.x * 2 + lax.div(q, 16), lax.div(fm, 2), lax.rem(fm, 2))
        pl.semaphore_signal(barrier, inc=1, device_id=device, device_id_type=MESH)

    for rx in (1, 3):
        pl.semaphore_signal(barrier, inc=1, device_id=me.at(rx=rx), device_id_type=MESH)
    pl.semaphore_wait(barrier, 33)

    keep = pltpu.make_async_copy(tok, xfull.at[me.fm], local_sem.at[0])
    swap = sends.make(tok, xfull.at[me.fm], me.across(1 - me.c))

    @pl.when(me.n == 0)
    def _():
        keep.start()

    @pl.when(me.n == 1)
    def _():
        swap.start()

    def exchange(k):
        t = lax.rem(me.fm + k, 16)
        return pltpu.make_async_remote_copy(
            src_ref=wpk.at[t],
            dst_ref=wown.at[me.fm],
            send_sem=ex_send.at[k],
            recv_sem=ex_recv.at[k],
            device_id=(me.dp, lax.div(t, 2), lax.rem(t, 2)),
            device_id_type=MESH,
        )

    @pl.loop(1, 16)
    def _(k):
        exchange(k).start()

    own = pltpu.make_async_copy(wpk.at[me.fm], wown.at[me.fm], local_sem.at[1])
    own.start()

    def tell(k):
        q = lax.rem(me.c * 8 + me.fs + k, 16)
        return pltpu.make_async_remote_copy(
            src_ref=small,
            dst_ref=sfull.at[me.fm],
            send_sem=small_send.at[k],
            recv_sem=small_recv.at[me.fm],
            device_id=(me.x * 2 + lax.div(q, 8), lax.rem(q, 8), me.c),
            device_id_type=MESH,
        )

    note = pltpu.make_async_copy(small, sfull.at[me.fm], local_sem.at[2])

    @pl.when(me.n == 1)
    def _():
        tell(0).start()

    @pl.when(me.n == 0)
    def _():
        note.start()

    @pl.loop(1, 16)
    def _(k):
        tell(k).start()

    @pl.when(me.n == 0)
    def _():
        keep.wait()

    @pl.when(me.n == 1)
    def _():
        swap.wait_recv()

    blocks = BlockGather(me, xfull, sends)
    blocks.first()

    own.wait()

    @pl.loop(1, 16)
    def _(k):
        exchange(k).wait_recv()

    far = pltpu.make_async_remote_copy(
        src_ref=wown,
        dst_ref=wfull.at[me.dp],
        send_sem=ex_send.at[16],
        recv_sem=ex_recv.at[16 + me.c],
        device_id=me.across(me.g),
        device_id_type=MESH,
    )
    far.start()
    near = pltpu.make_async_remote_copy(
        src_ref=wown,
        dst_ref=wfull.at[me.dp],
        send_sem=ex_send.at[17],
        recv_sem=ex_recv.at[18],
        device_id=me.twin(),
        device_id_type=MESH,
    )
    stay = pltpu.make_async_copy(wown, wfull.at[me.dp], local_sem.at[3])

    @pl.when(me.n == 1)
    def _():
        near.start()

    @pl.when(me.n == 0)
    def _():
        stay.start()

    blocks.second()

    def from_core(core):
        return pltpu.make_async_remote_copy(
            src_ref=wown,
            dst_ref=wfull.at[me.dp],
            send_sem=ex_send.at[16],
            recv_sem=ex_recv.at[16 + core],
            device_id=me.across(me.g),
            device_id_type=MESH,
        )

    @pl.when(me.n == 1)
    def _():
        from_core(0).wait_recv()
        from_core(1).wait_recv()

    @pl.when(me.n == 0)
    def _():
        near.wait_recv()
        stay.wait()

    right, left = me.at(rx=1), me.at(rx=3)
    pair = wfull.at[pl.ds(me.x * 2, 2)]
    to_right = sends.start(pair, pair, right)
    to_left = sends.start(pair, pair, left)
    blocks.third()
    blocks.fourth()
    to_right.wait_recv()
    first = wfull.at[lax.rem(me.x + 3, 4) * 2]
    on_right = sends.start(first, first, right)
    to_left.wait_recv()
    second = wfull.at[lax.rem(me.x + 1, 4) * 2 + 1]
    on_left = sends.start(second, second, left)
    blocks.last()
    on_right.wait_recv()
    on_left.wait_recv()

    @pl.loop(0, 16)
    def _(j):
        @pl.when(jnp.logical_or(me.n == 1, j != me.fm))
        def _():
            pltpu.make_async_remote_copy(
                src_ref=small,
                dst_ref=sfull.at[j],
                send_sem=small_send.at[0],
                recv_sem=small_recv.at[j],
                device_id=me.twin(),
                device_id_type=MESH,
            ).wait_recv()

    @pl.loop(1, 16)
    def _(k):
        exchange(k).wait_send()
        tell(k).wait_send()

    far.wait_send()

    @pl.when(me.n == 1)
    def _():
        tell(0).wait_send()
        near.wait_send()
        swap.wait_send()

    @pl.when(me.n == 0)
    def _():
        note.wait()

    sends.finish()


def params(collective_id):
    return pltpu.CompilerParams(
        collective_id=collective_id, has_side_effects=True, vmem_limit_bytes=60 * 2**20
    )


def gather_inputs(tokens, small, wpk):
    rows, width = tokens.shape
    return pl.pallas_call(
        gather_kernel,
        name="gather_inputs",
        out_shape=(
            jax.ShapeDtypeStruct((16, rows, width), tokens.dtype),
            jax.ShapeDtypeStruct((16, *small.shape), small.dtype),
            jax.ShapeDtypeStruct((8, *wpk.shape), wpk.dtype),
        ),
        in_specs=[VMEM] * 3,
        out_specs=(ANY, VMEM, ANY),
        scratch_shapes=[
            pltpu.VMEM(wpk.shape, wpk.dtype),
            pltpu.SemaphoreType.DMA((40,)),
            pltpu.SemaphoreType.DMA((40,)),
            pltpu.SemaphoreType.DMA((4,)),
            pltpu.SemaphoreType.DMA((18,)),
            pltpu.SemaphoreType.DMA((19,)),
            pltpu.SemaphoreType.DMA((16,)),
            pltpu.SemaphoreType.DMA((16,)),
        ],
        compiler_params=params(0),
    )(tokens, small, wpk)


def gather_normed_kernel(block, full, send_sem, recv_sem, local_sem):
    me = Place()
    sends = Sends(send_sem, recv_sem)
    greet([me.at(ry=1), me.at(ry=3), me.at(rz=1), me.twin()])
    keep = pltpu.make_async_copy(block, full.at[me.slot(0, 0)], local_sem.at[0])
    keep.start()
    keep.wait()
    blocks = BlockGather(me, full, sends)
    blocks.first()
    blocks.second()
    blocks.third()
    blocks.fourth()
    blocks.last()
    sends.finish()


def gather_normed(block):
    return pl.pallas_call(
        gather_normed_kernel,
        name="gather_normed",
        out_shape=jax.ShapeDtypeStruct((16, *block.shape), block.dtype),
        in_specs=[VMEM],
        out_specs=ANY,
        scratch_shapes=[
            pltpu.SemaphoreType.DMA((32,)),
            pltpu.SemaphoreType.DMA((32,)),
            pltpu.SemaphoreType.DMA((1,)),
        ],
        compiler_params=params(1),
    )(block)


def add_rows(into, start, end, *others):
    @pl.loop(0, (end - start) // 16)
    def _(i):
        rows = pl.ds(pl.multiple_of(start + i * 16, 16), 16)
        total = into[rows].astype(jnp.float32)
        for other in others:
            total += other[pl.ds(pl.multiple_of(i * 16, 16), 16)].astype(jnp.float32)
        into[rows] = total.astype(into.dtype)


def scatter_kernel(
    part, hw, out, hwx, r, za, zb, fa0, fa1, ya, fb0, fb1, yb, send_sem, recv_sem, local_sem, hs, hr
):
    me = Place()
    sends = Sends(send_sem, recv_sem)
    up, down, over, twin = me.at(ry=1), me.at(ry=3), me.at(rz=1), me.twin()
    right, left, partner = me.at(rx=1), me.at(rx=3), me.across(me.c)
    greet([up, down, over, twin, right, left, partner])

    order = [(1, 2), (1, 0), (1, 1), (1, 3), (0, 2), (0, 1), (0, 3), (0, 0)]
    halves = [
        sends.start(part.at[me.other_slot(rz, ry)], r.at[rz * 4 + ry], twin) for rz, ry in order
    ]

    quarter = hw.shape[0] // 4
    half = quarter // 2

    def head_copy(k, start, size, device, src):
        rows = pl.ds(start, size)
        return pltpu.make_async_remote_copy(
            src_ref=src.at[rows],
            dst_ref=hwx.at[rows],
            send_sem=hs.at[k],
            recv_sem=hr.at[k],
            device_id=device,
            device_id_type=MESH,
        )

    head_out = head_copy(0, me.x * quarter, quarter, partner, hw)
    head_keep = pltpu.make_async_copy(hw, hwx, local_sem.at[0])
    head_right = head_copy(1, me.x * quarter, quarter, right, hwx)
    head_left = head_copy(2, me.x * quarter, quarter, left, hwx)
    head_right2 = head_copy(3, lax.rem(me.x + 3, 4) * quarter, half, right, hwx)
    head_left2 = head_copy(4, lax.rem(me.x + 1, 4) * quarter + half, half, left, hwx)

    @pl.when(me.n == 0)
    def _():
        head_out.start()
        head_keep.start()

    a_got, b_got, y_got = {}, {}, {}
    for (rz, ry), copy in zip(order, halves):
        copy.wait_recv()
        block = r.at[rz * 4 + ry]
        add_rows(block, 0, 128, part.at[me.slot(rz, ry)])
        if rz == 1:
            a_got[ry] = sends.start(block.at[pl.ds(0, A_END)], za.at[ry], over)
        if ry == 2:
            b_got[rz, 0] = sends.start(block.at[pl.ds(A_END, B_MID - A_END)], fb0.at[rz], up)
            b_got[rz, 1] = sends.start(block.at[pl.ds(B_MID, 128 - B_MID)], fb1.at[rz], down)

    @pl.when(me.n == 1)
    def _():
        head_out.wait_recv()
        head_right.start()
        head_left.start()

    tail = pl.ds(A_END, 128 - A_END)
    for rz in (1, 0):
        b_got[rz, 0].wait_recv()
        add_rows(r.at[rz * 4 + 1], A_END, B_MID, fb0.at[rz])
        y_got[rz, 0] = sends.start(r.at[rz * 4 + 1, tail], yb.at[rz * 2], up)
        b_got[rz, 1].wait_recv()
        add_rows(r.at[rz * 4 + 3], B_MID, 128, fb1.at[rz])
        y_got[rz, 1] = sends.start(r.at[rz * 4 + 3, tail], yb.at[rz * 2 + 1], down)

    head = pl.ds(0, A_END)
    a_got[2].wait_recv()
    add_rows(r.at[2], 0, A_END, za.at[2])
    f_up = sends.start(r.at[2, pl.ds(0, A_MID)], fa0, up)
    f_down = sends.start(r.at[2, pl.ds(A_MID, A_END - A_MID)], fa1, down)

    y_got[1, 0].wait_recv()
    y_got[1, 1].wait_recv()
    add_rows(r.at[4], A_END, 128, yb.at[2], yb.at[3])
    z_got = sends.start(r.at[4, tail], zb, over)

    @pl.when(me.n == 1)
    def _():
        head_right.wait_recv()
        head_right2.start()
        head_left.wait_recv()
        head_left2.start()

    a_got[1].wait_recv()
    add_rows(r.at[1], 0, A_END, za.at[1])
    f_up.wait_recv()
    add_rows(r.at[1], 0, A_MID, fa0)
    g_up = sends.start(r.at[1, head], ya.at[0], up)
    a_got[3].wait_recv()
    add_rows(r.at[3], 0, A_END, za.at[3])
    f_down.wait_recv()
    add_rows(r.at[3], A_MID, A_END, fa1)
    g_down = sends.start(r.at[3, head], ya.at[1], down)

    def total(start, end, others):
        @pl.loop(0, (end - start) // 16)
        def _(i):
            here = pl.ds(pl.multiple_of(i * 16, 16), 16)
            rows = pl.ds(pl.multiple_of(start + i * 16, 16), 16)
            value = r[0, rows].astype(jnp.float32)
            for other in others:
                value += other[here].astype(jnp.float32)
            out[rows] = value

    y_got[0, 0].wait_recv()
    y_got[0, 1].wait_recv()
    z_got.wait_recv()
    total(A_END, 128, [yb.at[0], yb.at[1], zb])
    a_got[0].wait_recv()
    g_up.wait_recv()
    g_down.wait_recv()
    total(0, A_END, [za.at[0], ya.at[0], ya.at[1]])

    @pl.when(me.n == 1)
    def _():
        head_right2.wait_recv()
        head_left2.wait_recv()
        head_right.wait_send()
        head_left.wait_send()
        head_right2.wait_send()
        head_left2.wait_send()

    @pl.when(me.n == 0)
    def _():
        head_out.wait_send()
        head_keep.wait()

    sends.finish()


def scatter_parts(part, hw):
    blocks, rows, width = part.shape
    dtype = part.dtype
    return pl.pallas_call(
        scatter_kernel,
        name="scatter_parts",
        out_shape=(
            jax.ShapeDtypeStruct((rows, width), jnp.float32),
            jax.ShapeDtypeStruct(hw.shape, hw.dtype),
        ),
        in_specs=[VMEM, ANY],
        out_specs=(VMEM, ANY),
        scratch_shapes=[
            pltpu.VMEM((8, rows, width), dtype),
            pltpu.VMEM((4, A_END, width), dtype),
            pltpu.VMEM((rows - A_END, width), dtype),
            pltpu.VMEM((A_MID, width), dtype),
            pltpu.VMEM((A_END - A_MID, width), dtype),
            pltpu.VMEM((2, A_END, width), dtype),
            pltpu.VMEM((2, B_MID - A_END, width), dtype),
            pltpu.VMEM((2, rows - B_MID, width), dtype),
            pltpu.VMEM((4, rows - A_END, width), dtype),
            pltpu.SemaphoreType.DMA((32,)),
            pltpu.SemaphoreType.DMA((32,)),
            pltpu.SemaphoreType.DMA((1,)),
            pltpu.SemaphoreType.DMA((5,)),
            pltpu.SemaphoreType.DMA((5,)),
        ],
        compiler_params=params(2),
    )(part, hw)


def totals_kernel(stats, got, send_sem, recv_sem, local_sem):
    me = Place()
    barrier = pltpu.get_barrier_semaphore()
    mine = me.c * 16 + me.fm

    @pl.loop(1, 32)
    def _(k):
        q = lax.rem(mine + k, 32)
        fm = lax.rem(q, 16)
        device = (me.x * 2 + lax.div(q, 16), lax.div(fm, 2), lax.rem(fm, 2))
        pl.semaphore_signal(barrier, inc=1, device_id=device, device_id_type=MESH)

    pl.semaphore_wait(barrier, 31)
    sender = me.c * 8 + me.fs

    def tell(k):
        b = lax.rem(me.fm + k, 16)
        return pltpu.make_async_remote_copy(
            src_ref=stats.at[b],
            dst_ref=got.at[sender],
            send_sem=send_sem.at[k],
            recv_sem=recv_sem.at[sender],
            device_id=(me.x * 2 + me.g, lax.div(b, 2), lax.rem(b, 2)),
            device_id_type=MESH,
        )

    note = pltpu.make_async_copy(stats.at[me.fm], got.at[sender], local_sem.at[0])

    @pl.when(me.n == 1)
    def _():
        tell(0).start()

    @pl.when(me.n == 0)
    def _():
        note.start()

    @pl.loop(1, 16)
    def _(k):
        tell(k).start()

    @pl.loop(0, 16)
    def _(j):
        @pl.when(jnp.logical_or(me.n == 1, j != sender))
        def _():
            pltpu.make_async_remote_copy(
                src_ref=stats.at[0],
                dst_ref=got.at[j],
                send_sem=send_sem.at[0],
                recv_sem=recv_sem.at[j],
                device_id=me.twin(),
                device_id_type=MESH,
            ).wait_recv()

    @pl.loop(1, 16)
    def _(k):
        tell(k).wait_send()

    @pl.when(me.n == 1)
    def _():
        tell(0).wait_send()

    @pl.when(me.n == 0)
    def _():
        note.wait()


def exchange_totals(stats):
    return pl.pallas_call(
        totals_kernel,
        name="exchange_totals",
        out_shape=jax.ShapeDtypeStruct(stats.shape, stats.dtype),
        in_specs=[VMEM],
        out_specs=VMEM,
        scratch_shapes=[
            pltpu.SemaphoreType.DMA((16,)),
            pltpu.SemaphoreType.DMA((16,)),
            pltpu.SemaphoreType.DMA((1,)),
        ],
        compiler_params=params(3),
    )(stats)


def copy_for_each(value, axis):
    copies = jnp.broadcast_to(value, (lax.axis_size(axis), *value.shape))
    return lax.all_to_all(copies, axis, split_axis=0, concat_axis=0, tiled=True)


def inverse_of(table):
    total_count = table.shape[0]
    places = jnp.arange(total_count, dtype=jnp.int32)
    return jnp.sum(jnp.where(table[None, :] == places[:, None], places[None, :], 0), axis=1)


def pack_rows(stored, residues, fm_count):
    matrices, row_count, columns = stored.shape
    dp_count = residues.shape[0]
    split_rows = stored.reshape(
        matrices, row_count // dp_count, dp_count, fm_count, columns // fm_count
    )
    chosen = jnp.take(split_rows, residues, axis=2)
    return chosen.transpose(2, 3, 0, 1, 4).reshape(
        dp_count * fm_count, matrices, row_count // dp_count, columns // fm_count
    )


def unpack_rows(received, holder):
    ordered = jnp.take(received, holder, axis=0)
    devices, matrices, pair_rows, group_cols = ordered.shape
    return ordered.transpose(1, 0, 2, 3).reshape(matrices, devices * pair_rows, group_cols)


def everywhere(value):
    return lax.all_to_all(value, ("dp", "fsdp", "mp"), split_axis=0, concat_axis=0, tiled=True)


def forward(tokens_in, segment_ids, target_ids, old_weights, old_block, norm_gain, head_weight):
    me = Place()
    matrices, old_rows, columns = old_weights.shape
    groups = 16
    group_cols = columns // groups
    model_width = tokens_in.shape[1]

    by_group = old_weights.reshape(matrices, old_rows, groups, group_cols).transpose(2, 0, 1, 3)
    by_group = by_group.reshape(groups, matrices * old_rows, group_cols)
    number = jnp.broadcast_to(old_block.astype(jnp.bfloat16)[:, None, None], (groups, 8, group_cols))
    wpk = jnp.concatenate([by_group, number], axis=1)
    small = jnp.stack([segment_ids, target_ids] + [segment_ids] * 6)
    xfull, sfull, wfull = gather_inputs(tokens_in, small, wpk)

    wfull = wfull.reshape(128, *wpk.shape[1:])
    holder = inverse_of(wfull[:, matrices * old_rows, 0].astype(jnp.int32))
    logical = (
        jnp.take(wfull, holder, axis=0)[:, : matrices * old_rows]
        .reshape(128, matrices, old_rows, group_cols)
        .transpose(1, 0, 2, 3)
        .reshape(matrices, model_width, group_cols)
    )
    whole_tokens = xfull.reshape(-1, model_width)
    segments = sfull[:, 0].reshape(-1)
    targets = sfull[:, 1].reshape(-1)
    seq_len = whole_tokens.shape[0]

    projected = jnp.einsum(
        "sd,mdc->msc", whole_tokens, logical[:3], preferred_element_type=jnp.float32
    )
    heads = group_cols // HD
    queries = projected[0].astype(jnp.bfloat16).reshape(seq_len, heads, HD)
    keys_all = projected[1].astype(jnp.bfloat16).reshape(seq_len, heads, HD)
    values_all = projected[2].astype(jnp.bfloat16).reshape(seq_len, heads, HD)
    positions_all = jnp.arange(seq_len, dtype=jnp.int32)
    allowed = (positions_all[:, None] >= positions_all[None, :]) & (
        segments[:, None] == segments[None, :]
    )
    scores = jnp.einsum("shd,thd->hst", queries, keys_all, preferred_element_type=jnp.float32) * (
        1.0 / math.sqrt(HD)
    )
    scores = jnp.where(allowed[None], scores, -1e30)
    row_max = jnp.max(scores, axis=2, keepdims=True)
    expo = jnp.where(allowed[None], jnp.exp(scores - row_max), 0.0)
    soft = (expo / jnp.sum(expo, axis=2, keepdims=True)).astype(jnp.bfloat16)
    attended = jnp.einsum("hst,thd->shd", soft, values_all, preferred_element_type=jnp.float32)
    attended = attended.astype(jnp.bfloat16).reshape(seq_len, group_cols)
    partial_value = jnp.einsum(
        "sc,dc->sd", attended, logical[3], preferred_element_type=jnp.float32
    )
    partial_value = partial_value.astype(jnp.bfloat16).reshape(16, 128, model_width)
    summed, heads_used = scatter_parts(partial_value, head_weight)

    own = me.slot(0, 0)
    hidden = lax.dynamic_index_in_dim(xfull, own, 0, keepdims=False).astype(jnp.float32) + summed
    scale = lax.rsqrt(jnp.mean(hidden * hidden, axis=1, keepdims=True) + 1e-05)
    normed = (hidden * scale * norm_gain).astype(jnp.bfloat16)
    nfull = gather_normed(normed).reshape(seq_len, model_width)

    logits = jnp.dot(nfull, heads_used, preferred_element_type=jnp.float32)
    vocab_dev = logits.shape[1]
    row_top = jnp.max(logits, axis=1)
    row_total = jnp.sum(jnp.exp(logits - row_top[:, None]), axis=1)
    vocab_ids = jnp.arange(vocab_dev, dtype=jnp.int32) + own * vocab_dev
    picked = jnp.sum(jnp.where(vocab_ids[None, :] == targets[:, None], logits, 0.0), axis=1)
    stats = jnp.stack([row_top, row_total, picked] + [picked] * 5).reshape(8, 16, 128)
    got = exchange_totals(stats.transpose(1, 0, 2))
    top = jnp.max(got[:, 0], axis=0)
    total = jnp.sum(got[:, 1] * jnp.exp(got[:, 0] - top), axis=0)
    loss = top + jnp.log(total) - jnp.sum(got[:, 2], axis=0)
    return loss, holder


def body(
    tokens_in,
    segment_ids,
    target_ids,
    old_weights,
    old_first,
    old_second,
    old_block,
    new_residue,
    norm_gain,
    head_weight,
):
    loss, holder = forward(
        tokens_in, segment_ids, target_ids, old_weights, old_block, norm_gain, head_weight
    )
    residues = copy_for_each(new_residue, "dp").reshape(-1)
    moments = jnp.concatenate(
        [pack_rows(old_first, residues, 16), pack_rows(old_second, residues, 16)], axis=1
    )
    got = everywhere(moments)
    new_first = unpack_rows(got[:, :4], holder)
    new_second = unpack_rows(got[:, 4:], holder)
    new_weights = unpack_rows(everywhere(pack_rows(old_weights, residues, 16)), holder)
    return (new_weights, new_first, new_second, loss)


def solution(mesh):
    placed = (
        P(("dp", "fsdp", "mp"), None),
        P(("dp", "fsdp", "mp")),
        P(("dp", "fsdp", "mp")),
        P(None, ("dp", "fsdp", "mp"), None),
        P(None, ("dp", "fsdp", "mp"), None),
        P(None, ("dp", "fsdp", "mp"), None),
        P(("dp", "fsdp", "mp")),
        P("dp"),
        P(),
        P(None, ("fsdp", "mp")),
    )
    return jax.shard_map(
        body,
        mesh=mesh,
        in_specs=placed,
        out_specs=(
            P(None, "dp", ("fsdp", "mp")),
            P(None, "dp", ("fsdp", "mp")),
            P(None, "dp", ("fsdp", "mp")),
            P(("dp", "fsdp", "mp")),
        ),
        check_vma=False,
    )
```

time: 799 us -> 546 us (0.68)
  blocking collectives: 408 us -> 0 us
  Pallas kernels: 0 us -> 362 us
  waiting for transfers between devices: 179 us -> 6.09 us
  starting transfers between devices: 32.9 us -> 16.1 us
  between operations: 16.4 us -> 2.73 us
    unnamed x1 -> x0, blocking collectives: 378 us -> none
    pallas_call x0 -> x4, Pallas kernels: none -> 362 us  [the longest x1 194 us: gather_normed(): pl.pallas_call(gather_normed_kernel, name='gather_normed', out_shape=jax....]
    psum x1 -> x0, waiting for transfers between devices: 127 us -> none  [body(): lax.psum(partial_value.astype(jnp.bfloat16), ('fsdp', 'mp'))]
    all_to_all x2, waiting for transfers between devices: 47.7 us -> 6.08 us  [everywhere(): lax.all_to_all(value, ('dp', 'fsdp', 'mp'), split_axis=0, concat_axis=0,...]
    all_gather x1 -> x0, blocking collectives: 30 us -> none  [turned_gather(): result = lax.all_gather(both, axis, axis=0, tiled=True)]
    all_to_all x2 -> x1, starting transfers between devices: 16.6 us -> 5.79 us  [copy_for_each(): return lax.all_to_all(copies, axis, split_axis=0, concat_axis=0, tiled=True)]
    reduce_sum x2 -> x3, other arithmetic: 15.6 us -> 6.66 us  [the longest x1 4.62 us: forward(): jnp.sum(jnp.where(vocab_ids[None, :] == targets[:, None], logits, 0.0), a...]
  transfers between devices with their start and end apart: 6 -> 3, of which waited for: 4 -> 1; matrix products, arithmetic and copies ran while one was open for 7% -> 25% of each run, Pallas kernels for 0% -> 68%
where the time goes in v1:
time: 546 us; the launch traced here: 537 us
  Pallas kernels  362 us (66%)
  matrix products  74.5 us (14%)
  local copies, waits for them, and re-layouts  47.2 us (9%)
  other arithmetic  27.7 us (5%)
  starting transfers between devices  16.1 us (3%)
  waiting for transfers between devices  6.09 us (1%)
    pallas_call x1, Pallas kernels, gather_normed(): pl.pallas_call(gather_normed_kernel, name='gather_normed', out_shape=jax....  194 us
    pallas_call x1, Pallas kernels, gather_inputs(): pl.pallas_call(gather_kernel, name='gather_inputs', out_shape=(jax.ShapeD...  94 us
    pallas_call x1, Pallas kernels, scatter_parts(): pl.pallas_call(scatter_kernel, name='scatter_parts', out_shape=(jax.Shape...  57.9 us
    sub x1, matrix products, forward(): expo = jnp.where(allowed[None], jnp.exp(scores - row_max), 0.0)  23.7 us
    dot_general x1, matrix products, forward(): logits = jnp.dot(nfull, heads_used, preferred_element_type=jnp.float32)  19 us
    pallas_call x1, Pallas kernels, exchange_totals(): pl.pallas_call(totals_kernel, name='exchange_totals', out_shape=jax.Shape...  16.9 us
    dot_general x1, matrix products, forward(): jnp.einsum('sd,mdc->msc', whole_tokens, logical[:3], preferred_element_ty...  13.1 us
    dot_general x1, matrix products, forward(): jnp.einsum('hst,thd->shd', soft, values_all, preferred_element_type=jnp.f...  12.2 us
  transfers between devices with their start and end apart: 3, of which 1 were waited for; matrix products, arithmetic and copies ran while one was open for 25% of the time, Pallas kernels for 68%

profile of v1, /device:TPU:1, one launch (start us, length us, event | category | flops | bytes accessed | tf_op | source)
XLA Modules:
  0.0 536.7 jit_solution(13149079165525929374)
XLA Ops:
  1.9 5.8 %all-to-all-start = ((s32[8,1,1]{2,1,0:T(1,128)}), s32[8,1,1]{2,1,0:T(1,128)S(1)}, u32[]{:S(2)}, u32[]{:S(2)}) async-start(s32[8,1,1]{2,1,0:T(1,128)} %broadcast_in_dim.109), calls=%async_computation | async-start | bytes 8192 | tf_op jit(solution)/shard_map/all_to_all | solution.py:681
  8.3 1.2 copy.116
  9.5 1.5 stack.16.small
  11.1 1.0 concatenate.7.wpk
  12.0 94.0 %gather_inputs.1 = (bf16[16,128,3072]{2,1,0:T(8,128)(2,1)}, s32[16,8,128]{2,1,0:T(8,128)}, bf16[8,16,104,256]{3,2,1,0:T(8,128)(2,1)}) custom-call(bf16[128,3072]{1,0:T(8,128)(2,1)} %tok.1, s32[8,128]{1,0:T(8,128)} %stack.16.small, bf16[16,104,256]{2,1,0:T(8,128)(2,1)} %concatenate.7.wpk), custom_call_target="tpu_custom_call" | custom-call | tf_op jit(solution)/shard_map/gather_inputs/pallas_call | solution.py:368
  106.1 1.0 slice.79
  107.3 6.8 %gather_fusion.2 = bf16[128,104,256]{2,1,0:T(8,128)(2,1)} fusion(bf16[128,104,256]{2,1,0:T(8,128)(2,1)} %bitcast.106, s32[1024]{0:T(1024)S(1)} %pad_clamp_fusion.2), kind=kCustom, calls=%fused_computation.6 | custom fusion | bytes 13632000 | tf_op jit(solution)/shard_map/jit(_take)/gather | solution.py:729
  114.1 3.4 slice_select_fusion
  117.7 2.5 slice.83
  120.2 1.1 copy.112
  121.2 3.2 copy.113
  124.9 0.9 fusion.18
  126.2 13.1 %fusion.9 = bf16[3,2048,256]{1,2,0:T(8,128)(2,1)S(1)} fusion(bf16[3,3072,256]{2,1,0:T(8,128)(2,1)S(1)} %bitcast.114, bf16[2048,3072,1]{1,0,2:T(8,128)(2,1)} %bitcast.134), kind=kOutput, calls=%fused_computation.25 | convolution fusion | flops 9665249280 | bytes 20447232 | tf_op jit(solution)/shard_map/sd,mdc->msc/dot_general | solution.py:739
  139.3 1.7 fusion.15
  141.0 5.4 %fusion.4 = pred[2048,2048]{0,1:T(8,128)(4,1)} fusion(s32[2048]{0:T(1024)S(1)} %bitcast.135), kind=kLoop, calls=%fused_computation.15 | loop fusion | flops 12582912 | bytes 4202496 | tf_op jit(solution)/shard_map/and | solution.py:747
  146.4 23.7 %fusion.19 = (f32[2,2048]{1,0:T(2,128)S(1)}, f32[2,2048,2048]{1,2,0:T(8,128)}) fusion(pred[2048,2048]{0,1:T(8,128)(4,1)} %fusion.4, bf16[2048,2,128]{0,2,1:T(8,128)(2,1)} %bitcast.126, bf16[2048,2,128]{0,2,1:T(8,128)(2,1)} %bitcast.125), kind=kOutput, calls=%fused_computation.63 | convolution fusion | flops 2189428736 | bytes 39862272 | tf_op jit(solution)/shard_map/sub | solution.py:755
  170.1 12.2 %fusion.10 = bf16[2,128,2048]{2,1,0:T(8,128)(2,1)S(1)} fusion(bf16[2048,2,128]{0,2,1:T(8,128)(2,1)} %bitcast.124, f32[2,2048,2048]{1,2,0:T(8,128)} %get-tuple-element.53, f32[2,2048]{1,0:T(2,128)S(1)} %get-tuple-element.52), kind=kOutput, calls=%fused_computation.26 | convolution fusion | flops 2164785152 | bytes 35667968 | tf_op jit(solution)/shard_map/hst,thd->shd/dot_general | solution.py:757
  182.3 6.5 %convolution_convert_fusion = bf16[2048,3072]{1,0:T(8,128)(2,1)} fusion(bf16[2048,256]{0,1:T(8,128)(2,1)S(1)} %bitcast.121, bf16[3072,256]{1,0:T(8,128)(2,1)S(1)} %bitcast.107), kind=kOutput, calls=%fused_computation.18 | convolution fusion | flops 3227516928 | bytes 15204352 | tf_op jit(solution)/shard_map/sc,dc->sd/dot_general | solution.py:759
  188.8 57.9 %scatter_parts.1 = (f32[128,3072]{1,0:T(8,128)}, bf16[3072,1024]{1,0:T(8,128)(2,1)}) custom-call(bf16[16,128,3072]{2,1,0:T(8,128)(2,1)} %bitcast.101, bf16[3072,1024]{1,0:T(8,128)(2,1)} %hw.1), custom_call_target="tpu_custom_call" | custom-call | tf_op jit(solution)/shard_map/scatter_parts/pallas_call | solution.py:568
  246.7 2.0 multiply_reduce_fusion
  248.8 2.3 multiply_convert_fusion.block
  251.1 193.6 %gather_normed.1 = bf16[16,128,3072]{2,1,0:T(8,128)(2,1)} custom-call(bf16[128,3072]{1,0:T(8,128)(2,1)} %multiply_convert_fusion.block), custom_call_target="tpu_custom_call" | custom-call | tf_op jit(solution)/shard_map/gather_normed/pallas_call | solution.py:409
  445.0 1.5 gather_fusion
  446.5 1.4 select_bitcast_fusion.2
  448.0 1.5 copy.91
  449.5 6.1 %all-to-all-start.1 = ((bf16[128,4,3,256]{3,1,2,0:T(4,128)(2,1)}), bf16[128,4,3,256]{3,1,2,0:T(4,128)(2,1)}, u32[]{:S(2)}, u32[]{:S(2)}) async-start(bf16[128,4,3,256]{3,1,2,0:T(4,128)(2,1)} %copy.91), calls=%async_computation.1 | async-start | bytes 1572864 | tf_op jit(solution)/shard_map/all_to_all | solution.py:709
  455.6 1.8 gather_fusion.3
  457.4 1.8 gather_fusion.4
  459.2 1.8 select_bitcast_fusion.1
  461.2 1.0 copy.94
  462.3 1.0 copy.95
  463.3 2.4 pad_maximum_fusion
  465.7 6.1 %all-to-all-done.1 = bf16[128,4,3,256]{3,1,2,0:T(4,128)(2,1)} async-done(((bf16[128,4,3,256]{3,1,2,0:T(4,128)(2,1)}), bf16[128,4,3,256]{3,1,2,0:T(4,128)(2,1)}, u32[]{:S(2)}, u32[]{:S(2)}) %all-to-all-start.1) | async-done | bytes 786464 | tf_op jit(solution)/shard_map/all_to_all | solution.py:709
  471.8 4.3 all-to-all-start.2
  476.1 19.0 %fusion.20 = (f32[2048]{0:T(1024)S(1)}, f32[2048,1024]{0,1:T(8,128)}) fusion(bf16[2048,3072]{1,0:T(8,128)(2,1)} %bitcast.104, bf16[3072,1024]{1,0:T(8,128)(2,1)} %get-tuple-element.15), kind=kOutput, calls=%fused_computation.64 | convolution fusion | flops 12886996992 | bytes 27271168 | tf_op jit(solution)/shard_map/dot_general | solution.py:771
  495.1 4.6 select_reduce_fusion
  499.7 0.7 stack.38
  500.4 16.9 %exchange_totals.1 = f32[16,8,128]{2,1,0:T(8,128)} custom-call(f32[16,8,128]{2,1,0:T(8,128)} %bitcast.133), custom_call_target="tpu_custom_call" | custom-call | tf_op jit(solution)/shard_map/exchange_totals/pallas_call | solution.py:664
  517.3 1.0 fusion.17
  518.9 3.2 gather_fusion.1
  522.1 1.6 broadcast_select_fusion.2
  523.7 1.0 copy.102
  524.7 2.1 fusion.16
  526.8 2.9 gather_fusion.6
  529.7 2.9 gather_fusion.5
  532.7 0.8 broadcast_select_fusion
  533.4 1.4 copy.104
  534.8 1.4 copy.103
  (48 shorter events, 3.0 us)
Async XLA Ops:
  1.9 442.9 %all-to-all-start = ((s32[8,1,1]{2,1,0:T(1,128)}), s32[8,1,1]{2,1,0:T(1,128)S(1)}, u32[]{:S(2)}, u32[]{:S(2)}) async-start(s32[8,1,1]{2,1,0:T(1,128)} %broadcast_in_dim.109), calls=%async_computation | async-start | bytes 8192 | tf_op jit(solution)/shard_map/all_to_all | solution.py:681
  107.3 6.8 %copy-start.8 = (s32[128]{0:T(128)}, s32[128]{0:T(128)S(1)}, u32[]{:S(2)}) copy-start(s32[128]{0:T(128)S(1)} %select_reduce_fusion.1) | copy-start | bytes 1540
  117.7 2.5 copy-start.4
  120.2 4.2 copy-start.6
  121.2 4.6 copy-start
  188.8 59.9 %copy-start.7 = (f32[3072]{0:T(1024)S(1)}, f32[3072]{0:T(1024)}, u32[]{:S(2)}) copy-start(f32[3072]{0:T(1024)} %param.22) | copy-start | bytes 36868
  246.7 2.1 copy-start.1
  251.1 193.9 %copy-start.5 = (bf16[12,8,16,256]{3,2,1,0:T(8,128)(2,1)S(1)}, bf16[12,8,16,256]{3,2,1,0:T(8,128)(2,1)}, u32[]{:S(2)}) copy-start(bf16[12,8,16,256]{3,2,1,0:T(8,128)(2,1)} %copy.112) | copy-start | bytes 2359300
  446.5 9.1 %copy-start.2 = (f32[12,8,16,256]{3,2,1,0:T(8,128)S(1)}, f32[12,8,16,256]{3,2,1,0:T(8,128)}, u32[]{:S(2)}) copy-start(f32[12,8,16,256]{3,2,1,0:T(8,128)} %copy.113) | copy-start | bytes 4718596
  449.5 22.3 %all-to-all-start.1 = ((bf16[128,4,3,256]{3,1,2,0:T(4,128)(2,1)}), bf16[128,4,3,256]{3,1,2,0:T(4,128)(2,1)}, u32[]{:S(2)}, u32[]{:S(2)}) async-start(bf16[128,4,3,256]{3,1,2,0:T(4,128)(2,1)} %copy.91), calls=%async_computation.1 | async-start | bytes 1572864 | tf_op jit(solution)/shard_map/all_to_all | solution.py:709
  457.4 1.8 copy-start.3
  471.8 52.9 %all-to-all-start.2 = ((f32[128,8,3,256]{3,1,2,0:T(8,128)}), f32[128,8,3,256]{3,1,2,0:T(8,128)S(1)}, u32[]{:S(2)}, u32[]{:S(2)}) async-start(f32[128,8,3,256]{3,1,2,0:T(8,128)} %pad_maximum_fusion), calls=%async_computation.2 | async-start | bytes 6291456 | tf_op jit(solution)/shard_map/all_to_all | solution.py:709
  495.1 23.2 %copy-start.9 = (s32[128]{0:T(128)S(1)}, s32[128]{0:T(128)}, u32[]{:S(2)}) copy-start(s32[128]{0:T(128)} %copy-done.8) | copy-start | bytes 1540

commit v2 on v1

--- a/solution.py
+++ b/solution.py
@@ -1,4 +1,3 @@
-import functools
 import math
 
 import jax
@@ -87,6 +86,21 @@
     pl.semaphore_wait(barrier, len(devices))
 
 
+def greet_plane(me, extra=()):
+    barrier = pltpu.get_barrier_semaphore()
+
+    @pl.loop(1, 32)
+    def _(k):
+        q = lax.rem(me.c * 16 + me.fm + k, 32)
+        fm = lax.rem(q, 16)
+        device = (me.x * 2 + lax.div(q, 16), lax.div(fm, 2), lax.rem(fm, 2))
+        pl.semaphore_signal(barrier, inc=1, device_id=device, device_id_type=MESH)
+
+    for device in extra:
+        pl.semaphore_signal(barrier, inc=1, device_id=device, device_id_type=MESH)
+    pl.semaphore_wait(barrier, 31 + len(extra))
+
+
 class BlockGather:
     def __init__(self, me, full, sends):
         self.me, self.full, self.sends, self.got, self.twins = me, full, sends, {}, []
@@ -156,11 +170,13 @@
 
 
 def gather_kernel(
+    holder,
     tok,
     small,
     wpk,
     xfull,
     sfull,
+    wlog,
     wfull,
     wown,
     send_sem,
@@ -173,20 +189,7 @@
 ):
     me = Place()
     sends = Sends(send_sem, recv_sem)
-    mine = me.c * 16 + me.fm
-
-    barrier = pltpu.get_barrier_semaphore()
-
-    @pl.loop(1, 32)
-    def _(k):
-        q = lax.rem(mine + k, 32)
-        fm = lax.rem(q, 16)
-        device = (me.x * 2 + lax.div(q, 16), lax.div(fm, 2), lax.rem(fm, 2))
-        pl.semaphore_signal(barrier, inc=1, device_id=device, device_id_type=MESH)
-
-    for rx in (1, 3):
-        pl.semaphore_signal(barrier, inc=1, device_id=me.at(rx=rx), device_id_type=MESH)
-    pl.semaphore_wait(barrier, 33)
+    greet_plane(me, [me.at(rx=1), me.at(rx=3)])
 
     keep = pltpu.make_async_copy(tok, xfull.at[me.fm], local_sem.at[0])
     swap = sends.make(tok, xfull.at[me.fm], me.across(1 - me.c))
@@ -261,7 +264,7 @@
 
     far = pltpu.make_async_remote_copy(
         src_ref=wown,
-        dst_ref=wfull.at[me.dp],
+        dst_ref=wfull.at[pl.ds(me.dp * 16, 16)],
         send_sem=ex_send.at[16],
         recv_sem=ex_recv.at[16 + me.c],
         device_id=me.across(me.g),
@@ -270,13 +273,13 @@
     far.start()
     near = pltpu.make_async_remote_copy(
         src_ref=wown,
-        dst_ref=wfull.at[me.dp],
+        dst_ref=wfull.at[pl.ds(me.dp * 16, 16)],
         send_sem=ex_send.at[17],
         recv_sem=ex_recv.at[18],
         device_id=me.twin(),
         device_id_type=MESH,
     )
-    stay = pltpu.make_async_copy(wown, wfull.at[me.dp], local_sem.at[3])
+    stay = pltpu.make_async_copy(wown, wfull.at[pl.ds(me.dp * 16, 16)], local_sem.at[3])
 
     @pl.when(me.n == 1)
     def _():
@@ -291,7 +294,7 @@
     def from_core(core):
         return pltpu.make_async_remote_copy(
             src_ref=wown,
-            dst_ref=wfull.at[me.dp],
+            dst_ref=wfull.at[pl.ds(me.dp * 16, 16)],
             send_sem=ex_send.at[16],
             recv_sem=ex_recv.at[16 + core],
             device_id=me.across(me.g),
@@ -309,20 +312,30 @@
         stay.wait()
 
     right, left = me.at(rx=1), me.at(rx=3)
-    pair = wfull.at[pl.ds(me.x * 2, 2)]
+    pair = wfull.at[pl.ds(me.x * 32, 32)]
     to_right = sends.start(pair, pair, right)
     to_left = sends.start(pair, pair, left)
     blocks.third()
     blocks.fourth()
     to_right.wait_recv()
-    first = wfull.at[lax.rem(me.x + 3, 4) * 2]
+    first = wfull.at[pl.ds(lax.rem(me.x + 3, 4) * 32, 16)]
     on_right = sends.start(first, first, right)
     to_left.wait_recv()
-    second = wfull.at[lax.rem(me.x + 1, 4) * 2 + 1]
+    second = wfull.at[pl.ds(lax.rem(me.x + 1, 4) * 32 + 16, 16)]
     on_left = sends.start(second, second, left)
     blocks.last()
     on_right.wait_recv()
     on_left.wait_recv()
+
+    rows = wpk.shape[1] // 4
+
+    @pl.loop(0, 128)
+    def _(b):
+        where = holder[b]
+        for m in range(4):
+            wlog[m, pl.ds(pl.multiple_of(b * rows, 8), rows)] = wfull[
+                where, pl.ds(m * rows, rows)
+            ]
 
     @pl.loop(0, 16)
     def _(j):
@@ -363,19 +376,21 @@
     )
 
 
-def gather_inputs(tokens, small, wpk):
+def gather_inputs(holder, tokens, small, wpk):
     rows, width = tokens.shape
+    old_rows = wpk.shape[1] // 4
     return pl.pallas_call(
         gather_kernel,
         name="gather_inputs",
         out_shape=(
             jax.ShapeDtypeStruct((16, rows, width), tokens.dtype),
             jax.ShapeDtypeStruct((16, *small.shape), small.dtype),
-            jax.ShapeDtypeStruct((8, *wpk.shape), wpk.dtype),
+            jax.ShapeDtypeStruct((4, 128 * old_rows, wpk.shape[2]), wpk.dtype),
         ),
-        in_specs=[VMEM] * 3,
-        out_specs=(ANY, VMEM, ANY),
+        in_specs=[pl.BlockSpec(memory_space=pltpu.SMEM)] + [VMEM] * 3,
+        out_specs=(ANY, VMEM, VMEM),
         scratch_shapes=[
+            pltpu.VMEM((128, *wpk.shape[1:]), wpk.dtype),
             pltpu.VMEM(wpk.shape, wpk.dtype),
             pltpu.SemaphoreType.DMA((40,)),
             pltpu.SemaphoreType.DMA((40,)),
@@ -386,39 +401,7 @@
             pltpu.SemaphoreType.DMA((16,)),
         ],
         compiler_params=params(0),
-    )(tokens, small, wpk)
-
-
-def gather_normed_kernel(block, full, send_sem, recv_sem, local_sem):
-    me = Place()
-    sends = Sends(send_sem, recv_sem)
-    greet([me.at(ry=1), me.at(ry=3), me.at(rz=1), me.twin()])
-    keep = pltpu.make_async_copy(block, full.at[me.slot(0, 0)], local_sem.at[0])
-    keep.start()
-    keep.wait()
-    blocks = BlockGather(me, full, sends)
-    blocks.first()
-    blocks.second()
-    blocks.third()
-    blocks.fourth()
-    blocks.last()
-    sends.finish()
-
-
-def gather_normed(block):
-    return pl.pallas_call(
-        gather_normed_kernel,
-        name="gather_normed",
-        out_shape=jax.ShapeDtypeStruct((16, *block.shape), block.dtype),
-        in_specs=[VMEM],
-        out_specs=ANY,
-        scratch_shapes=[
-            pltpu.SemaphoreType.DMA((32,)),
-            pltpu.SemaphoreType.DMA((32,)),
-            pltpu.SemaphoreType.DMA((1,)),
-        ],
-        compiler_params=params(1),
-    )(block)
+    )(holder, tokens, small, wpk)
 
 
 def add_rows(into, start, end, *others):
@@ -432,7 +415,7 @@
 
 
 def scatter_kernel(
-    part, hw, out, hwx, r, za, zb, fa0, fa1, ya, fb0, fb1, yb, send_sem, recv_sem, local_sem, hs, hr
+    att, w3, hw, out, hwx, parts, r, za, zb, fa0, fa1, ya, fb0, fb1, yb, send_sem, recv_sem, local_sem, hs, hr
 ):
     me = Place()
     sends = Sends(send_sem, recv_sem)
@@ -441,10 +424,6 @@
     greet([up, down, over, twin, right, left, partner])
 
     order = [(1, 2), (1, 0), (1, 1), (1, 3), (0, 2), (0, 1), (0, 3), (0, 0)]
-    halves = [
-        sends.start(part.at[me.other_slot(rz, ry)], r.at[rz * 4 + ry], twin) for rz, ry in order
-    ]
-
     quarter = hw.shape[0] // 4
     half = quarter // 2
 
@@ -471,11 +450,46 @@
         head_out.start()
         head_keep.start()
 
+    def project(slot, write):
+        @pl.loop(0, out.shape[1] // 512)
+        def _(i):
+            part = pl.ds(pl.multiple_of(i * 512, 512), 512)
+            write(
+                part,
+                lax.dot_general(
+                    att[slot],
+                    w3[part],
+                    (((1,), (1,)), ((), ())),
+                    preferred_element_type=jnp.float32,
+                ),
+            )
+
+    def halve(rz, ry):
+        j = rz * 4 + ry
+
+        def write(part, value):
+            parts[j, :, part] = value.astype(parts.dtype)
+
+        project(me.other_slot(rz, ry), write)
+        return sends.start(parts.at[j], r.at[j], twin)
+
+    def merge(rz, ry):
+        j = rz * 4 + ry
+
+        def write(part, value):
+            total = r[j, :, part].astype(jnp.float32) + value
+            r[j, :, part] = total.astype(r.dtype)
+
+        project(me.slot(rz, ry), write)
+
     a_got, b_got, y_got = {}, {}, {}
-    for (rz, ry), copy in zip(order, halves):
-        copy.wait_recv()
+    halves = [halve(*order[0]), halve(*order[1])]
+    for at, (rz, ry) in enumerate(order):
+        if at + 2 < 8:
+            halves.append(halve(*order[at + 2]))
+        halves[at].wait_recv()
         block = r.at[rz * 4 + ry]
-        add_rows(block, 0, 128, part.at[me.slot(rz, ry)])
+        merge(rz, ry)
         if rz == 1:
             a_got[ry] = sends.start(block.at[pl.ds(0, A_END)], za.at[ry], over)
         if ry == 2:
@@ -562,9 +576,9 @@
     sends.finish()
 
 
-def scatter_parts(part, hw):
-    blocks, rows, width = part.shape
-    dtype = part.dtype
+def scatter_parts(att, w3, hw):
+    rows, width = att.shape[1], w3.shape[0]
+    dtype = att.dtype
     return pl.pallas_call(
         scatter_kernel,
         name="scatter_parts",
@@ -572,9 +586,10 @@
             jax.ShapeDtypeStruct((rows, width), jnp.float32),
             jax.ShapeDtypeStruct(hw.shape, hw.dtype),
         ),
-        in_specs=[VMEM, ANY],
+        in_specs=[VMEM] * 3,
         out_specs=(VMEM, ANY),
         scratch_shapes=[
+            pltpu.VMEM((8, rows, width), dtype),
             pltpu.VMEM((8, rows, width), dtype),
             pltpu.VMEM((4, A_END, width), dtype),
             pltpu.VMEM((rows - A_END, width), dtype),
@@ -591,94 +606,254 @@
             pltpu.SemaphoreType.DMA((5,)),
         ],
         compiler_params=params(2),
-    )(part, hw)
-
-
-def totals_kernel(stats, got, send_sem, recv_sem, local_sem):
+    )(att, w3, hw)
+
+
+def finish_kernel(
+    summed,
+    xown,
+    gain,
+    hw,
+    tcol,
+    loss,
+    full,
+    lg,
+    cols,
+    st,
+    got,
+    send_sem,
+    recv_sem,
+    local_sem,
+    tell_send,
+    tell_recv,
+):
     me = Place()
-    barrier = pltpu.get_barrier_semaphore()
-    mine = me.c * 16 + me.fm
-
-    @pl.loop(1, 32)
-    def _(k):
-        q = lax.rem(mine + k, 32)
-        fm = lax.rem(q, 16)
-        device = (me.x * 2 + lax.div(q, 16), lax.div(fm, 2), lax.rem(fm, 2))
-        pl.semaphore_signal(barrier, inc=1, device_id=device, device_id_type=MESH)
-
-    pl.semaphore_wait(barrier, 31)
+    sends = Sends(send_sem, recv_sem)
+    greet_plane(me)
+    own = me.slot(0, 0)
+    width = summed.shape[1]
+
+    @pl.loop(0, 8)
+    def _(i):
+        rows = pl.ds(pl.multiple_of(i * 16, 16), 16)
+        hidden = xown[rows].astype(jnp.float32) + summed[rows]
+        mean = jnp.sum(hidden * hidden, axis=1, keepdims=True) * (1.0 / width)
+        normed = hidden * lax.rsqrt(mean + 1e-05) * gain[...]
+        full[own, rows] = normed.astype(full.dtype)
+
+    blocks = BlockGather(me, full, sends)
+    vocab = hw.shape[1]
     sender = me.c * 8 + me.fs
 
-    def tell(k):
-        b = lax.rem(me.fm + k, 16)
+    def tell(b):
         return pltpu.make_async_remote_copy(
-            src_ref=stats.at[b],
+            src_ref=st.at[b],
             dst_ref=got.at[sender],
-            send_sem=send_sem.at[k],
-            recv_sem=recv_sem.at[sender],
+            send_sem=tell_send.at[b],
+            recv_sem=tell_recv.at[sender],
             device_id=(me.x * 2 + me.g, lax.div(b, 2), lax.rem(b, 2)),
             device_id_type=MESH,
         )
 
-    note = pltpu.make_async_copy(stats.at[me.fm], got.at[sender], local_sem.at[0])
-
-    @pl.when(me.n == 1)
-    def _():
-        tell(0).start()
-
-    @pl.when(me.n == 0)
-    def _():
-        note.start()
-
-    @pl.loop(1, 16)
-    def _(k):
-        tell(k).start()
+    note = pltpu.make_async_copy(st.at[me.fm], got.at[sender], local_sem.at[0])
+
+    def score(rz, ry):
+        slots = (me.slot(rz, ry), me.other_slot(rz, ry))
+
+        @pl.loop(0, vocab // 256)
+        def _(i):
+            part = pl.ds(pl.multiple_of(i * 256, 256), 256)
+            pair = jnp.concatenate([full[slots[0]], full[slots[1]]], axis=0)
+            lg[:, part] = jnp.dot(pair, hw[:, part], preferred_element_type=jnp.float32)
+
+        for t, slot in enumerate(slots):
+
+            @pl.loop(0, 8)
+            def _(i):
+                here = pl.ds(pl.multiple_of(t * 128 + i * 16, 16), 16)
+                rows = pl.ds(pl.multiple_of(i * 16, 16), 16)
+                logits = lg[here]
+                top = jnp.max(logits, axis=1, keepdims=True)
+                total = jnp.sum(jnp.exp(logits - top), axis=1, keepdims=True)
+                ids = lax.broadcasted_iota(jnp.int32, logits.shape, 1) + own * vocab
+                picked = jnp.sum(
+                    jnp.where(ids == tcol[slot, rows], logits, 0.0), axis=1, keepdims=True
+                )
+                lane = lax.broadcasted_iota(jnp.int32, (16, 128), 1)
+                cols[rows] = jnp.where(lane == 0, top, jnp.where(lane == 1, total, picked))
+
+            st[slot] = cols[...].T[:8]
+
+            @pl.when(jnp.logical_or(me.n == 1, slot != me.fm))
+            def _():
+                tell(slot).start()
+
+            @pl.when(jnp.logical_and(me.n == 0, slot == me.fm))
+            def _():
+                note.start()
+
+    blocks.first()
+    blocks.twins[0].wait_recv()
+    score(0, 0)
+    blocks.second()
+    blocks.third()
+    blocks.twins[1].wait_recv()
+    score(0, 1)
+    blocks.fourth()
+    blocks.twins[2].wait_recv()
+    score(0, 3)
+    blocks.twins[3].wait_recv()
+    score(1, 0)
+    blocks.wait("bf0", "bf1")
+    blocks.share(0, 2)
+    blocks.twins[4].wait_recv()
+    score(1, 1)
+    blocks.wait("az2", "bf2", "bf3")
+    blocks.share(1, 2)
+    blocks.twins[5].wait_recv()
+    score(1, 3)
+    blocks.twins[6].wait_recv()
+    score(0, 2)
+    blocks.twins[7].wait_recv()
+    score(1, 2)
 
     @pl.loop(0, 16)
     def _(j):
         @pl.when(jnp.logical_or(me.n == 1, j != sender))
         def _():
             pltpu.make_async_remote_copy(
-                src_ref=stats.at[0],
+                src_ref=st.at[0],
                 dst_ref=got.at[j],
-                send_sem=send_sem.at[0],
-                recv_sem=recv_sem.at[j],
+                send_sem=tell_send.at[0],
+                recv_sem=tell_recv.at[j],
                 device_id=me.twin(),
                 device_id_type=MESH,
             ).wait_recv()
 
-    @pl.loop(1, 16)
-    def _(k):
-        tell(k).wait_send()
-
-    @pl.when(me.n == 1)
-    def _():
-        tell(0).wait_send()
-
     @pl.when(me.n == 0)
     def _():
         note.wait()
 
-
-def exchange_totals(stats):
+    top = got[0, 0:1]
+    for j in range(1, 16):
+        top = jnp.maximum(top, got[j, 0:1])
+    total, picked = jnp.zeros_like(top), jnp.zeros_like(top)
+    for j in range(16):
+        total += got[j, 1:2] * jnp.exp(got[j, 0:1] - top)
+        picked += got[j, 2:3]
+    loss[...] = jnp.broadcast_to(top + jnp.log(total) - picked, loss.shape)
+
+    @pl.loop(0, 16)
+    def _(b):
+        @pl.when(jnp.logical_or(me.n == 1, b != me.fm))
+        def _():
+            tell(b).wait_send()
+
+    sends.finish()
+
+
+def finish(summed, xown, gain, hw, tcol):
+    rows, width = summed.shape
     return pl.pallas_call(
-        totals_kernel,
-        name="exchange_totals",
-        out_shape=jax.ShapeDtypeStruct(stats.shape, stats.dtype),
-        in_specs=[VMEM],
+        finish_kernel,
+        name="finish",
+        out_shape=jax.ShapeDtypeStruct((8, rows), jnp.float32),
+        in_specs=[VMEM] * 5,
         out_specs=VMEM,
         scratch_shapes=[
+            pltpu.VMEM((16, rows, width), jnp.bfloat16),
+            pltpu.VMEM((2 * rows, hw.shape[1]), jnp.float32),
+            pltpu.VMEM((rows, 128), jnp.float32),
+            pltpu.VMEM((16, 8, rows), jnp.float32),
+            pltpu.VMEM((16, 8, rows), jnp.float32),
+            pltpu.SemaphoreType.DMA((32,)),
+            pltpu.SemaphoreType.DMA((32,)),
+            pltpu.SemaphoreType.DMA((1,)),
             pltpu.SemaphoreType.DMA((16,)),
             pltpu.SemaphoreType.DMA((16,)),
-            pltpu.SemaphoreType.DMA((1,)),
         ],
-        compiler_params=params(3),
-    )(stats)
-
-
-def copy_for_each(value, axis):
-    copies = jnp.broadcast_to(value, (lax.axis_size(axis), *value.shape))
-    return lax.all_to_all(copies, axis, split_axis=0, concat_axis=0, tiled=True)
+        compiler_params=params(1),
+    )(summed, xown, gain, hw, tcol)
+
+
+def attend_kernel(x, w, seg_row, seg_col, out, q, k, vt):
+    heads = out.shape[1] // HD
+    seq = x.shape[0]
+    size = 256
+
+    @pl.loop(0, seq // size)
+    def _(i):
+        rows = pl.ds(pl.multiple_of(i * size, size), size)
+        block = x[rows]
+        q[rows] = jnp.dot(block, w[0], preferred_element_type=jnp.float32).astype(q.dtype)
+        k[rows] = jnp.dot(block, w[1], preferred_element_type=jnp.float32).astype(k.dtype)
+        v = jnp.dot(block, w[2], preferred_element_type=jnp.float32)
+        vt[:, rows] = v.T.astype(vt.dtype)
+
+    scale = math.log2(math.e) / math.sqrt(HD)
+
+    @pl.loop(0, seq // size)
+    def _(i):
+        rows = pl.ds(pl.multiple_of(i * size, size), size)
+        own = seg_row[0:1, rows]
+        ahead = lax.broadcasted_iota(jnp.int32, (size, size), 0) - lax.broadcasted_iota(
+            jnp.int32, (size, size), 1
+        )
+
+        def step(j, carry):
+            cols = pl.ds(pl.multiple_of(j * size, size), size)
+            allowed = (ahead <= (i - j) * size) & (seg_col[cols] == own)
+            result = []
+            for h in range(heads):
+                part = pl.ds(h * HD, HD)
+                top, total, acc = carry[h]
+                score = lax.dot_general(
+                    k[cols, part],
+                    q[rows, part],
+                    (((1,), (1,)), ((), ())),
+                    preferred_element_type=jnp.float32,
+                )
+                score = jnp.where(allowed, score * scale, -1e30)
+                new_top = jnp.maximum(top, jnp.max(score, axis=0, keepdims=True))
+                prob = jnp.exp2(score - new_top)
+                keep = jnp.exp2(top - new_top)
+                total = total * keep + jnp.sum(prob, axis=0, keepdims=True)
+                acc = acc * keep + jnp.dot(
+                    vt[part, cols], prob.astype(vt.dtype), preferred_element_type=jnp.float32
+                )
+                result.append((new_top, total, acc))
+            return tuple(result)
+
+        start = (
+            jnp.full((1, size), -1e30, jnp.float32),
+            jnp.zeros((1, size), jnp.float32),
+            jnp.zeros((HD, size), jnp.float32),
+        )
+        done = lax.fori_loop(0, i + 1, step, (start,) * heads)
+        for h in range(heads):
+            _, total, acc = done[h]
+            out[rows, pl.ds(h * HD, HD)] = (acc / total).T.astype(out.dtype)
+
+
+def attend(x, w, segments):
+    seq = x.shape[0]
+    cols = w.shape[2]
+    return pl.pallas_call(
+        attend_kernel,
+        name="attend",
+        out_shape=jax.ShapeDtypeStruct((seq, cols), x.dtype),
+        in_specs=[VMEM] * 4,
+        out_specs=VMEM,
+        scratch_shapes=[
+            pltpu.VMEM((seq, cols), x.dtype),
+            pltpu.VMEM((seq, cols), x.dtype),
+            pltpu.VMEM((cols, seq), x.dtype),
+        ],
+        compiler_params=pltpu.CompilerParams(vmem_limit_bytes=60 * 2**20),
+        cost_estimate=pl.CostEstimate(
+            flops=30 * 10**9, bytes_accessed=20 * 2**20, transcendentals=4 * 10**6
+        ),
+    )(x, w, segments[None, :], segments[:, None])
 
 
 def inverse_of(table):
@@ -707,79 +882,6 @@
 
 def everywhere(value):
     return lax.all_to_all(value, ("dp", "fsdp", "mp"), split_axis=0, concat_axis=0, tiled=True)
-
-
-def forward(tokens_in, segment_ids, target_ids, old_weights, old_block, norm_gain, head_weight):
-    me = Place()
-    matrices, old_rows, columns = old_weights.shape
-    groups = 16
-    group_cols = columns // groups
-    model_width = tokens_in.shape[1]
-
-    by_group = old_weights.reshape(matrices, old_rows, groups, group_cols).transpose(2, 0, 1, 3)
-    by_group = by_group.reshape(groups, matrices * old_rows, group_cols)
-    number = jnp.broadcast_to(old_block.astype(jnp.bfloat16)[:, None, None], (groups, 8, group_cols))
-    wpk = jnp.concatenate([by_group, number], axis=1)
-    small = jnp.stack([segment_ids, target_ids] + [segment_ids] * 6)
-    xfull, sfull, wfull = gather_inputs(tokens_in, small, wpk)
-
-    wfull = wfull.reshape(128, *wpk.shape[1:])
-    holder = inverse_of(wfull[:, matrices * old_rows, 0].astype(jnp.int32))
-    logical = (
-        jnp.take(wfull, holder, axis=0)[:, : matrices * old_rows]
-        .reshape(128, matrices, old_rows, group_cols)
-        .transpose(1, 0, 2, 3)
-        .reshape(matrices, model_width, group_cols)
-    )
-    whole_tokens = xfull.reshape(-1, model_width)
-    segments = sfull[:, 0].reshape(-1)
-    targets = sfull[:, 1].reshape(-1)
-    seq_len = whole_tokens.shape[0]
-
-    projected = jnp.einsum(
-        "sd,mdc->msc", whole_tokens, logical[:3], preferred_element_type=jnp.float32
-    )
-    heads = group_cols // HD
-    queries = projected[0].astype(jnp.bfloat16).reshape(seq_len, heads, HD)
-    keys_all = projected[1].astype(jnp.bfloat16).reshape(seq_len, heads, HD)
-    values_all = projected[2].astype(jnp.bfloat16).reshape(seq_len, heads, HD)
-    positions_all = jnp.arange(seq_len, dtype=jnp.int32)
-    allowed = (positions_all[:, None] >= positions_all[None, :]) & (
-        segments[:, None] == segments[None, :]
-    )
-    scores = jnp.einsum("shd,thd->hst", queries, keys_all, preferred_element_type=jnp.float32) * (
-        1.0 / math.sqrt(HD)
-    )
-    scores = jnp.where(allowed[None], scores, -1e30)
-    row_max = jnp.max(scores, axis=2, keepdims=True)
-    expo = jnp.where(allowed[None], jnp.exp(scores - row_max), 0.0)
-    soft = (expo / jnp.sum(expo, axis=2, keepdims=True)).astype(jnp.bfloat16)
-    attended = jnp.einsum("hst,thd->shd", soft, values_all, preferred_element_type=jnp.float32)
-    attended = attended.astype(jnp.bfloat16).reshape(seq_len, group_cols)
-    partial_value = jnp.einsum(
-        "sc,dc->sd", attended, logical[3], preferred_element_type=jnp.float32
-    )
-    partial_value = partial_value.astype(jnp.bfloat16).reshape(16, 128, model_width)
-    summed, heads_used = scatter_parts(partial_value, head_weight)
-
-    own = me.slot(0, 0)
-    hidden = lax.dynamic_index_in_dim(xfull, own, 0, keepdims=False).astype(jnp.float32) + summed
-    scale = lax.rsqrt(jnp.mean(hidden * hidden, axis=1, keepdims=True) + 1e-05)
-    normed = (hidden * scale * norm_gain).astype(jnp.bfloat16)
-    nfull = gather_normed(normed).reshape(seq_len, model_width)
-
-    logits = jnp.dot(nfull, heads_used, preferred_element_type=jnp.float32)
-    vocab_dev = logits.shape[1]
-    row_top = jnp.max(logits, axis=1)
-    row_total = jnp.sum(jnp.exp(logits - row_top[:, None]), axis=1)
-    vocab_ids = jnp.arange(vocab_dev, dtype=jnp.int32) + own * vocab_dev
-    picked = jnp.sum(jnp.where(vocab_ids[None, :] == targets[:, None], logits, 0.0), axis=1)
-    stats = jnp.stack([row_top, row_total, picked] + [picked] * 5).reshape(8, 16, 128)
-    got = exchange_totals(stats.transpose(1, 0, 2))
-    top = jnp.max(got[:, 0], axis=0)
-    total = jnp.sum(got[:, 1] * jnp.exp(got[:, 0] - top), axis=0)
-    loss = top + jnp.log(total) - jnp.sum(got[:, 2], axis=0)
-    return loss, holder
 
 
 def body(
@@ -794,17 +896,48 @@
     norm_gain,
     head_weight,
 ):
-    loss, holder = forward(
-        tokens_in, segment_ids, target_ids, old_weights, old_block, norm_gain, head_weight
-    )
-    residues = copy_for_each(new_residue, "dp").reshape(-1)
+    me = Place()
+    matrices, old_rows, columns = old_weights.shape
+    groups = 16
+    group_cols = columns // groups
+    model_width = tokens_in.shape[1]
+
+    tables = everywhere(jnp.broadcast_to(jnp.stack([old_block, new_residue], 1), (128, 2)))
+    holder = inverse_of(tables[:, 0])
+    residues = tables[::groups, 1]
+
+    by_group = old_weights.reshape(matrices, old_rows, groups, group_cols).transpose(2, 0, 1, 3)
+    by_group = by_group.reshape(groups, matrices * old_rows, group_cols)
+    small = jnp.stack([segment_ids, target_ids] + [segment_ids] * 6)
+    xfull, sfull, weights = gather_inputs(holder, tokens_in, small, by_group)
+
+    whole_tokens = xfull.reshape(-1, model_width)
+    segments = sfull[:, 0].reshape(-1)
+    targets = sfull[:, 1][:, :, None]
+    own = me.slot(0, 0)
+    xown = lax.dynamic_index_in_dim(xfull, own, 0, keepdims=False)
+
+    first, second, stored, weights = lax.optimization_barrier(
+        (old_first, old_second, old_weights, weights)
+    )
     moments = jnp.concatenate(
-        [pack_rows(old_first, residues, 16), pack_rows(old_second, residues, 16)], axis=1
-    )
-    got = everywhere(moments)
-    new_first = unpack_rows(got[:, :4], holder)
-    new_second = unpack_rows(got[:, 4:], holder)
-    new_weights = unpack_rows(everywhere(pack_rows(old_weights, residues, 16)), holder)
+        [pack_rows(first, residues, groups), pack_rows(second, residues, groups)], axis=1
+    )
+    got_moments = everywhere(moments)
+    got_weights = everywhere(pack_rows(stored, residues, groups))
+
+    attended = attend(whole_tokens, weights[:3], segments)
+    attended, got_moments, got_weights = lax.optimization_barrier(
+        (attended, got_moments, got_weights)
+    )
+    summed, heads_used = scatter_parts(
+        attended.reshape(16, -1, group_cols), weights[3], head_weight
+    )
+    loss = finish(summed, xown, norm_gain[None, :], heads_used, targets)[0]
+
+    new_first = unpack_rows(got_moments[:, :matrices], holder)
+    new_second = unpack_rows(got_moments[:, matrices:], holder)
+    new_weights = unpack_rows(got_weights, holder)
     return (new_weights, new_first, new_second, loss)
 
 

time: 546 us -> 377 us (0.69); the launches traced: 537 us -> 376 us
  Pallas kernels: 362 us -> 283 us
  matrix products: 74.5 us -> 0 us
  other arithmetic: 27.7 us -> 8.32 us
  starting transfers between devices: 16.1 us -> 25 us
    pallas_call x2, Pallas kernels: 210 us -> 130 us  [the longest x1 83 us: finish(): pl.pallas_call(finish_kernel, name='finish', out_shape=jax.ShapeDtypeStru...]
    dot_general x4 -> x0, matrix products: 50.8 us -> none  [the longest x1 19 us: forward(): logits = jnp.dot(nfull, heads_used, preferred_element_type=jnp.float32)]
    sub x1 -> x0, matrix products: 23.7 us -> none  [forward(): expo = jnp.where(allowed[None], jnp.exp(scores - row_max), 0.0)]
    all_to_all x2 -> x3, starting transfers between devices: 10.3 us -> 25 us  [everywhere(): lax.all_to_all(value, ('dp', 'fsdp', 'mp'), split_axis=0, concat_axis=0,...]
    pallas_call x1, Pallas kernels: 57.9 us -> 65.6 us  [scatter_parts(): pl.pallas_call(scatter_kernel, name='scatter_parts', out_shape=(jax.Shape...]
    gather x1 -> x0, local copies, waits for them, and re-layouts: 6.78 us -> none  [forward(): jnp.take(wfull, holder, axis=0)[:, :matrices * old_rows]]
    pallas_call x1, Pallas kernels: 94 us -> 87.3 us  [gather_inputs(): pl.pallas_call(gather_kernel, name='gather_inputs', out_shape=(jax.ShapeD...]
    reduce_sum x3 -> x0, other arithmetic: 6.66 us -> none  [the longest x1 4.62 us: forward(): jnp.sum(jnp.where(vocab_ids[None, :] == targets[:, None], logits, 0.0), a...]
  transfers between devices with their start and end apart: 3 -> 3, of which waited for: 1 -> 2; matrix products, arithmetic and copies ran while one was open for 25% -> 5% of each run, Pallas kernels for 68% -> 12%
where the time goes in v2:
time: 377 us; the launch traced here: 376 us
  Pallas kernels  283 us (75%)
  local copies, waits for them, and re-layouts  47.2 us (13%)
  starting transfers between devices  25 us (7%)
  waiting for transfers between devices  10.8 us (3%)
  other arithmetic  8.32 us (2%)
    pallas_call x1, Pallas kernels, gather_inputs(): pl.pallas_call(gather_kernel, name='gather_inputs', out_shape=(jax.ShapeD...  87.3 us
    pallas_call x1, Pallas kernels, finish(): pl.pallas_call(finish_kernel, name='finish', out_shape=jax.ShapeDtypeStru...  83 us
    pallas_call x1, Pallas kernels, scatter_parts(): pl.pallas_call(scatter_kernel, name='scatter_parts', out_shape=(jax.Shape...  65.6 us
    pallas_call x1, Pallas kernels, attend(): pl.pallas_call(attend_kernel, name='attend', out_shape=jax.ShapeDtypeStru...  46.6 us
    all_to_all x3, starting transfers between devices, everywhere(): lax.all_to_all(value, ('dp', 'fsdp', 'mp'), split_axis=0, concat_axis=0,...  25 us
    all_to_all x3, waiting for transfers between devices, everywhere(): lax.all_to_all(value, ('dp', 'fsdp', 'mp'), split_axis=0, concat_axis=0,...  10.8 us
    gather x3, local copies, waits for them, and re-layouts, unpack_rows(): ordered = jnp.take(received, holder, axis=0)  9.05 us
  transfers between devices with their start and end apart: 3, of which 2 were waited for; matrix products, arithmetic and copies ran while one was open for 5% of the time, Pallas kernels for 12%

profile of v2, /device:TPU:1, one launch (start us, length us, event | category | flops | bytes accessed | tf_op | source)
XLA Modules:
  0.0 376.0 jit_solution(4762617704724218719)
XLA Ops:
  2.0 0.7 broadcast_in_dim.60
  2.7 11.5 %all-to-all-start = ((s32[128,1,2]{2,1,0:T(1,128)}), s32[128,1,2]{2,1,0:T(1,128)S(1)}, u32[]{:S(2)}, u32[]{:S(2)}) async-start(s32[128,1,2]{2,1,0:T(1,128)} %broadcast_in_dim.60), calls=%async_computation | async-start | bytes 131072 | tf_op jit(solution)/shard_map/all_to_all | solution.py:884
  14.2 2.2 copy.69
  16.4 0.6 stack.32.small
  17.1 6.9 %all-to-all-done = s32[128,1,2]{2,1,0:T(1,128)S(1)} async-done(((s32[128,1,2]{2,1,0:T(1,128)}), s32[128,1,2]{2,1,0:T(1,128)S(1)}, u32[]{:S(2)}, u32[]{:S(2)}) %all-to-all-start) | async-done | bytes 1056 | tf_op jit(solution)/shard_map/all_to_all | solution.py:884
  24.2 0.2 fusion
  24.4 0.1 and_reduce_fusion
  24.5 0.1 select_reduce_fusion.holder
  24.7 0.5 copy-done.5
  25.1 87.3 %gather_inputs.1 = (bf16[16,128,3072]{2,1,0:T(8,128)(2,1)}, s32[16,8,128]{2,1,0:T(8,128)}, bf16[4,3072,256]{2,1,0:T(8,128)(2,1)}) custom-call(s32[128]{0:T(128)} %copy-done.5, bf16[128,3072]{1,0:T(8,128)(2,1)} %tok.1, s32[8,128]{1,0:T(8,128)} %stack.32.small, bf16[16,96,256]{2,1,0:T(8,128)(2,1)} %bitcast.76), custom_call_target="tpu_custom_call" | custom-call | tf_op jit(solution)/shard_map/gather_inputs/pallas_call | solution.py:382
  112.4 1.5 fusion.3
  113.9 0.5 copy.65
  114.4 0.9 copy-done.3
  115.3 0.5 copy.66
  115.8 1.8 gather_fusion.2
  117.6 1.8 gather_fusion.3
  119.4 1.8 select_bitcast_fusion.1
  121.3 0.1 copy.55
  121.4 1.0 copy.57
  122.4 0.1 copy.54
  122.6 1.0 copy.56
  123.6 0.1 copy-done.1
  123.7 1.1 copy.67
  124.7 2.6 gather_fusion
  127.4 1.3 select_bitcast_fusion.2
  128.7 1.5 copy.59
  130.2 7.6 %all-to-all-start.2 = ((bf16[128,4,3,256]{3,1,2,0:T(4,128)(2,1)}), bf16[128,4,3,256]{3,1,2,0:T(4,128)(2,1)}, u32[]{:S(2)}, u32[]{:S(2)}) async-start(bf16[128,4,3,256]{3,1,2,0:T(4,128)(2,1)} %copy.59), calls=%async_computation.2 | async-start | bytes 1572864 | tf_op jit(solution)/shard_map/all_to_all | solution.py:884
  137.8 2.3 pad_maximum_fusion
  140.2 4.8 %slice.28.w = bf16[3,3072,256]{2,1,0:T(8,128)(2,1)} slice(bf16[4,3072,256]{2,1,0:T(8,128)(2,1)} %get-tuple-element.20), slice={[0:3], [0:3072], [0:256]} | slice | bytes 9437184 | tf_op jit(solution)/shard_map/slice | solution.py:929
  145.0 1.3 copy.53.seg_col
  146.3 1.4 copy.60.tcol
  147.7 2.6 slice_bitcast_fusion.w3
  150.3 3.9 %all-to-all-done.2 = bf16[128,4,3,256]{3,1,2,0:T(4,128)(2,1)} async-done(((bf16[128,4,3,256]{3,1,2,0:T(4,128)(2,1)}), bf16[128,4,3,256]{3,1,2,0:T(4,128)(2,1)}, u32[]{:S(2)}, u32[]{:S(2)}) %all-to-all-start.2) | async-done | bytes 786464 | tf_op jit(solution)/shard_map/all_to_all | solution.py:884
  154.2 5.9 %all-to-all-start.1 = ((f32[128,8,3,256]{3,1,2,0:T(8,128)}), f32[128,8,3,256]{3,1,2,0:T(8,128)S(1)}, u32[]{:S(2)}, u32[]{:S(2)}) async-start(f32[128,8,3,256]{3,1,2,0:T(8,128)} %pad_maximum_fusion), calls=%async_computation.1 | async-start | bytes 6291456 | tf_op jit(solution)/shard_map/all_to_all | solution.py:884
  160.1 2.1 dynamic-slice_bitcast_fusion.xown
  162.2 46.6 %attend.1 = bf16[2048,256]{1,0:T(8,128)(2,1)} custom-call(bf16[2048,3072]{1,0:T(8,128)(2,1)} %bitcast.85, bf16[3,3072,256]{2,1,0:T(8,128)(2,1)} %slice.28.w, s32[1,2048]{1,0:T(1,128)} %get-tuple-element.52.seg_row, s32[2048,1]{1,0:T(8,128)} %copy.53.seg_col), custom_call_target="tpu_custom_call" | custom-call | flops 30000001024 | bytes 20971520 | tf_op jit(solution)/shard_map/attend/pallas_call | solution.py:841
  208.8 3.2 gather_fusion.1
  212.0 1.6 broadcast_select_fusion.2
  213.6 1.0 copy.61
  214.6 2.1 fusion.2
  216.8 2.9 gather_fusion.5
  219.7 2.9 gather_fusion.4
  222.6 0.8 broadcast_select_fusion
  223.3 1.4 copy.62
  224.8 1.4 copy.63
  226.2 65.6 %scatter_parts.1 = (f32[128,3072]{1,0:T(8,128)}, bf16[3072,1024]{1,0:T(8,128)(2,1)}) custom-call(bf16[16,128,256]{2,1,0:T(8,128)(2,1)} %bitcast.82, bf16[3072,256]{1,0:T(8,128)(2,1)} %slice_bitcast_fusion.w3, bf16[3072,1024]{1,0:T(8,128)(2,1)} %hw.1), custom_call_target="tpu_custom_call" | custom-call | tf_op jit(solution)/shard_map/scatter_parts/pallas_call | solution.py:582
  291.8 83.0 %finish.1 = f32[8,128]{1,0:T(8,128)} custom-call(f32[128,3072]{1,0:T(8,128)} %get-tuple-element.28.summed, bf16[128,3072]{1,0:T(8,128)(2,1)} %dynamic-slice_bitcast_fusion.xown, f32[1,3072]{1,0:T(1,128)} %bitcast.94, bf16[3072,1024]{1,0:T(8,128)(2,1)} %get-tuple-element.29.hw, s32[16,128,1]{2,1,0:T(8,128)} %copy.60.tcol), custom_call_target="tpu_custom_call" | custom-call | tf_op jit(solution)/shard_map/finish/pallas_call | solution.py:757
  374.8 1.2 slice_bitcast_fusion.3
  (25 shorter events, 0.4 us)
Async XLA Ops:
  0.6 15.8 %copy-start.4 = (s32[128]{0:T(128)S(1)}, s32[128]{0:T(128)}, u32[]{:S(2)}) copy-start(s32[128]{0:T(128)} %param.15) | copy-start | bytes 1540
  0.6 15.8 %copy-start.6 = (s32[128]{0:T(128)S(1)}, s32[128]{0:T(128)}, u32[]{:S(2)}) copy-start(s32[128]{0:T(128)} %param.16) | copy-start | bytes 1540
  2.7 21.3 %all-to-all-start = ((s32[128,1,2]{2,1,0:T(1,128)}), s32[128,1,2]{2,1,0:T(1,128)S(1)}, u32[]{:S(2)}, u32[]{:S(2)}) async-start(s32[128,1,2]{2,1,0:T(1,128)} %broadcast_in_dim.60), calls=%async_computation | async-start | bytes 131072 | tf_op jit(solution)/shard_map/all_to_all | solution.py:884
  14.2 99.7 %copy-start.2 = (f32[4,24,4096]{2,1,0:T(8,128)S(1)}, f32[4,24,4096]{2,1,0:T(8,128)}, u32[]{:S(2)}) copy-start(f32[4,24,4096]{2,1,0:T(8,128)} %param.18) | copy-start | bytes 4718596
  24.6 0.5 copy-start.5
  113.9 1.4 copy-start.3
  117.6 1.8 copy-start
  122.5 1.1 copy-start.1
  130.2 24.0 %all-to-all-start.2 = ((bf16[128,4,3,256]{3,1,2,0:T(4,128)(2,1)}), bf16[128,4,3,256]{3,1,2,0:T(4,128)(2,1)}, u32[]{:S(2)}, u32[]{:S(2)}) async-start(bf16[128,4,3,256]{3,1,2,0:T(4,128)(2,1)} %copy.59), calls=%async_computation.2 | async-start | bytes 1572864 | tf_op jit(solution)/shard_map/all_to_all | solution.py:884
  154.2 54.6 %all-to-all-start.1 = ((f32[128,8,3,256]{3,1,2,0:T(8,128)}), f32[128,8,3,256]{3,1,2,0:T(8,128)S(1)}, u32[]{:S(2)}, u32[]{:S(2)}) async-start(f32[128,8,3,256]{3,1,2,0:T(8,128)} %pad_maximum_fusion), calls=%async_computation.1 | async-start | bytes 6291456 | tf_op jit(solution)/shard_map/all_to_all | solution.py:884

commit v3 on v2

--- a/solution.py
+++ b/solution.py
@@ -11,6 +11,7 @@
 MESH = pl.DeviceIdType.MESH
 A_END, A_MID, B_MID = 48, 32, 80
 VMEM = pl.BlockSpec(memory_space=pltpu.VMEM)
+SMEM = pl.BlockSpec(memory_space=pltpu.SMEM)
 ANY = pl.BlockSpec(memory_space=pl.ANY)
 
 
@@ -170,15 +171,18 @@
 
 
 def gather_kernel(
-    holder,
     tok,
     small,
+    mark,
     wpk,
     xfull,
     sfull,
     wlog,
+    tables,
     wfull,
     wown,
+    marks,
+    holder,
     send_sem,
     recv_sem,
     local_sem,
@@ -186,10 +190,19 @@
     ex_recv,
     small_send,
     small_recv,
+    mark_send,
+    mark_recv,
 ):
     me = Place()
     sends = Sends(send_sem, recv_sem)
-    greet_plane(me, [me.at(rx=1), me.at(rx=3)])
+    greet_plane(
+        me,
+        [
+            (lax.rem(me.x + rx, 4) * 2 + core, me.fs, me.g)
+            for rx in (1, 2, 3)
+            for core in (0, 1)
+        ],
+    )
 
     keep = pltpu.make_async_copy(tok, xfull.at[me.fm], local_sem.at[0])
     swap = sends.make(tok, xfull.at[me.fm], me.across(1 - me.c))
@@ -213,6 +226,37 @@
             device_id_type=MESH,
         )
 
+    place = me.dp * 16 + me.fm
+
+    def mark_plane(k):
+        t = lax.rem(me.fm + k, 16)
+        return pltpu.make_async_remote_copy(
+            src_ref=mark,
+            dst_ref=marks.at[place],
+            send_sem=mark_send.at[k],
+            recv_sem=mark_recv.at[k],
+            device_id=(me.dp, lax.div(t, 2), lax.rem(t, 2)),
+            device_id_type=MESH,
+        )
+
+    def mark_rest(k):
+        plane = marks.at[pl.ds(me.dp * 16, 16)]
+        return pltpu.make_async_remote_copy(
+            src_ref=plane,
+            dst_ref=plane,
+            send_sem=mark_send.at[16 + k],
+            recv_sem=mark_recv.at[16 + k],
+            device_id=(lax.rem(me.dp + k, 8), me.fs, me.g),
+            device_id_type=MESH,
+        )
+
+    mark_own = pltpu.make_async_copy(mark, marks.at[place], local_sem.at[4])
+    mark_own.start()
+
+    @pl.loop(1, 16)
+    def _(k):
+        mark_plane(k).start()
+
     @pl.loop(1, 16)
     def _(k):
         exchange(k).start()
@@ -255,6 +299,16 @@
 
     blocks = BlockGather(me, xfull, sends)
     blocks.first()
+
+    mark_own.wait()
+
+    @pl.loop(1, 16)
+    def _(k):
+        mark_plane(k).wait_recv()
+
+    @pl.loop(1, 8)
+    def _(k):
+        mark_rest(k).start()
 
     own.wait()
 
@@ -315,6 +369,25 @@
     pair = wfull.at[pl.ds(me.x * 32, 32)]
     to_right = sends.start(pair, pair, right)
     to_left = sends.start(pair, pair, left)
+
+    @pl.loop(1, 8)
+    def _(k):
+        mark_rest(k).wait_recv()
+
+    lane = lax.broadcasted_iota(jnp.int32, (8, 128), 1)
+    line = lax.broadcasted_iota(jnp.int32, (8, 128), 0)
+    found = lax.fori_loop(
+        0,
+        128,
+        lambda p, total: total + jnp.where(marks[p] == lane, p, 0),
+        jnp.zeros((8, 128), jnp.int32),
+    )
+    residues = jnp.zeros((8, 128), jnp.int32)
+    for i in range(8):
+        residues += jnp.where(lane == i, marks[i * 16], 0)
+    tables[...] = jnp.where(line == 0, jnp.minimum(found, 127), residues)
+    tell_scalar = pltpu.make_async_copy(tables, holder, local_sem.at[5])
+    tell_scalar.start()
     blocks.third()
     blocks.fourth()
     to_right.wait_recv()
@@ -328,10 +401,11 @@
     on_left.wait_recv()
 
     rows = wpk.shape[1] // 4
+    tell_scalar.wait()
 
     @pl.loop(0, 128)
     def _(b):
-        where = holder[b]
+        where = holder[0, b]
         for m in range(4):
             wlog[m, pl.ds(pl.multiple_of(b * rows, 8), rows)] = wfull[
                 where, pl.ds(m * rows, rows)
@@ -354,6 +428,11 @@
     def _(k):
         exchange(k).wait_send()
         tell(k).wait_send()
+        mark_plane(k).wait_send()
+
+    @pl.loop(1, 8)
+    def _(k):
+        mark_rest(k).wait_send()
 
     far.wait_send()
 
@@ -376,7 +455,7 @@
     )
 
 
-def gather_inputs(holder, tokens, small, wpk):
+def gather_inputs(tokens, small, mark, wpk):
     rows, width = tokens.shape
     old_rows = wpk.shape[1] // 4
     return pl.pallas_call(
@@ -386,22 +465,27 @@
             jax.ShapeDtypeStruct((16, rows, width), tokens.dtype),
             jax.ShapeDtypeStruct((16, *small.shape), small.dtype),
             jax.ShapeDtypeStruct((4, 128 * old_rows, wpk.shape[2]), wpk.dtype),
+            jax.ShapeDtypeStruct((8, 128), jnp.int32),
         ),
-        in_specs=[pl.BlockSpec(memory_space=pltpu.SMEM)] + [VMEM] * 3,
-        out_specs=(ANY, VMEM, VMEM),
+        in_specs=[VMEM] * 4,
+        out_specs=(ANY, VMEM, VMEM, VMEM),
         scratch_shapes=[
             pltpu.VMEM((128, *wpk.shape[1:]), wpk.dtype),
             pltpu.VMEM(wpk.shape, wpk.dtype),
+            pltpu.VMEM((128, 8, 128), jnp.int32),
+            pltpu.SMEM((8, 128), jnp.int32),
             pltpu.SemaphoreType.DMA((40,)),
             pltpu.SemaphoreType.DMA((40,)),
-            pltpu.SemaphoreType.DMA((4,)),
+            pltpu.SemaphoreType.DMA((6,)),
             pltpu.SemaphoreType.DMA((18,)),
             pltpu.SemaphoreType.DMA((19,)),
             pltpu.SemaphoreType.DMA((16,)),
             pltpu.SemaphoreType.DMA((16,)),
+            pltpu.SemaphoreType.DMA((24,)),
+            pltpu.SemaphoreType.DMA((24,)),
         ],
         compiler_params=params(0),
-    )(holder, tokens, small, wpk)
+    )(tokens, small, mark, wpk)
 
 
 def add_rows(into, start, end, *others):
@@ -415,7 +499,7 @@
 
 
 def scatter_kernel(
-    att, w3, hw, out, hwx, parts, r, za, zb, fa0, fa1, ya, fb0, fb1, yb, send_sem, recv_sem, local_sem, hs, hr
+    tables, att, w, hw, out, hwx, nw, tw, parts, r, za, zb, fa0, fa1, ya, fb0, fb1, yb, send_sem, recv_sem, local_sem, hs, hr
 ):
     me = Place()
     sends = Sends(send_sem, recv_sem)
@@ -458,7 +542,7 @@
                 part,
                 lax.dot_general(
                     att[slot],
-                    w3[part],
+                    w[3, part],
                     (((1,), (1,)), ((), ())),
                     preferred_element_type=jnp.float32,
                 ),
@@ -502,6 +586,28 @@
         head_right.start()
         head_left.start()
 
+    give = sends.make(tw, nw, twin)
+
+    @pl.when(me.n == 0)
+    def _():
+        lane = lax.broadcasted_iota(jnp.int32, (64, 256), 1)
+        line = lax.broadcasted_iota(jnp.int32, (64, 256), 0)
+        mine, other = tables[1, me.dp], tables[1, me.x * 2 + 1 - me.c]
+        wanted = jnp.where(line < 32, line * 8 + mine, (line - 32) * 8 + other)
+        pick = jnp.where(lane == wanted, 1.0, 0.0).astype(w.dtype)
+        for m in range(4):
+
+            @pl.loop(0, w.shape[1] // 256)
+            def _(t):
+                rows = pl.ds(pl.multiple_of(t * 256, 256), 256)
+                chosen = jnp.dot(pick, w[m, rows], preferred_element_type=jnp.float32)
+                chosen = chosen.astype(nw.dtype)
+                to = pl.ds(pl.multiple_of(t * 32, 32), 32)
+                nw[m, to] = chosen[:32]
+                tw[m, to] = chosen[32:]
+
+        give.start()
+
     tail = pl.ds(A_END, 128 - A_END)
     for rz in (1, 0):
         b_got[rz, 0].wait_recv()
@@ -561,6 +667,7 @@
 
     @pl.when(me.n == 1)
     def _():
+        give.wait_recv()
         head_right2.wait_recv()
         head_left2.wait_recv()
         head_right.wait_send()
@@ -570,14 +677,16 @@
 
     @pl.when(me.n == 0)
     def _():
+        give.wait_send()
         head_out.wait_send()
         head_keep.wait()
 
     sends.finish()
 
 
-def scatter_parts(att, w3, hw):
-    rows, width = att.shape[1], w3.shape[0]
+def scatter_parts(tables, att, w, hw):
+    rows, width = att.shape[1], w.shape[1]
+    kept = (w.shape[0], width // 8, w.shape[2])
     dtype = att.dtype
     return pl.pallas_call(
         scatter_kernel,
@@ -585,10 +694,12 @@
         out_shape=(
             jax.ShapeDtypeStruct((rows, width), jnp.float32),
             jax.ShapeDtypeStruct(hw.shape, hw.dtype),
+            jax.ShapeDtypeStruct(kept, w.dtype),
         ),
-        in_specs=[VMEM] * 3,
-        out_specs=(VMEM, ANY),
+        in_specs=[SMEM] + [VMEM] * 3,
+        out_specs=(VMEM, ANY, VMEM),
         scratch_shapes=[
+            pltpu.VMEM(kept, w.dtype),
             pltpu.VMEM((8, rows, width), dtype),
             pltpu.VMEM((8, rows, width), dtype),
             pltpu.VMEM((4, A_END, width), dtype),
@@ -606,7 +717,7 @@
             pltpu.SemaphoreType.DMA((5,)),
         ],
         compiler_params=params(2),
-    )(att, w3, hw)
+    )(tables, att, w, hw)
 
 
 def finish_kernel(
@@ -657,32 +768,39 @@
 
     note = pltpu.make_async_copy(st.at[me.fm], got.at[sender], local_sem.at[0])
 
-    def score(rz, ry):
-        slots = (me.slot(rz, ry), me.other_slot(rz, ry))
+    def score(*pairs):
+        slots = [slot(rz, ry) for rz, ry in pairs for slot in (me.slot, me.other_slot)]
+        rows = pl.ds(0, 128 * len(slots))
 
         @pl.loop(0, vocab // 256)
         def _(i):
             part = pl.ds(pl.multiple_of(i * 256, 256), 256)
-            pair = jnp.concatenate([full[slots[0]], full[slots[1]]], axis=0)
-            lg[:, part] = jnp.dot(pair, hw[:, part], preferred_element_type=jnp.float32)
+            block = jnp.concatenate([full[slot] for slot in slots], axis=0)
+            lg[rows, part] = jnp.dot(block, hw[:, part], preferred_element_type=jnp.float32)
 
         for t, slot in enumerate(slots):
 
-            @pl.loop(0, 8)
+            @pl.loop(0, 4)
             def _(i):
-                here = pl.ds(pl.multiple_of(t * 128 + i * 16, 16), 16)
-                rows = pl.ds(pl.multiple_of(i * 16, 16), 16)
-                logits = lg[here]
-                top = jnp.max(logits, axis=1, keepdims=True)
-                total = jnp.sum(jnp.exp(logits - top), axis=1, keepdims=True)
-                ids = lax.broadcasted_iota(jnp.int32, logits.shape, 1) + own * vocab
-                picked = jnp.sum(
-                    jnp.where(ids == tcol[slot, rows], logits, 0.0), axis=1, keepdims=True
-                )
-                lane = lax.broadcasted_iota(jnp.int32, (16, 128), 1)
-                cols[rows] = jnp.where(lane == 0, top, jnp.where(lane == 1, total, picked))
-
-            st[slot] = cols[...].T[:8]
+                here = pl.ds(pl.multiple_of(t * 128 + i * 32, 32), 32)
+                to = pl.ds(pl.multiple_of(i * 32, 32), 32)
+                parts = [lg[here, pl.ds(j * 128, 128)] for j in range(vocab // 128)]
+                top = parts[0]
+                for part in parts[1:]:
+                    top = jnp.maximum(top, part)
+                wanted = tcol[slot, to] - own * vocab
+                ids = lax.broadcasted_iota(jnp.int32, top.shape, 1)
+                total, picked = jnp.zeros_like(top), jnp.zeros_like(top)
+                for j, part in enumerate(parts):
+                    total += jnp.exp(part - top)
+                    picked += jnp.where(ids + j * 128 == wanted, part, 0.0)
+                cols[0, to], cols[1, to], cols[2, to] = top, total, picked
+
+            tops = cols[0].T
+            top = jnp.max(tops, axis=0, keepdims=True)
+            total = jnp.sum(cols[1].T * jnp.exp(tops - top), axis=0, keepdims=True)
+            picked = jnp.sum(cols[2].T, axis=0, keepdims=True)
+            st[slot] = jnp.concatenate([top, total, picked, jnp.zeros((5, 128))], axis=0)
 
             @pl.when(jnp.logical_or(me.n == 1, slot != me.fm))
             def _():
@@ -692,30 +810,28 @@
             def _():
                 note.start()
 
+    def twins(*which):
+        for k in which:
+            blocks.twins[k].wait_recv()
+
     blocks.first()
-    blocks.twins[0].wait_recv()
-    score(0, 0)
+    twins(0)
+    score((0, 0))
     blocks.second()
     blocks.third()
-    blocks.twins[1].wait_recv()
-    score(0, 1)
+    twins(1, 2)
+    score((0, 1), (0, 3))
     blocks.fourth()
-    blocks.twins[2].wait_recv()
-    score(0, 3)
-    blocks.twins[3].wait_recv()
-    score(1, 0)
     blocks.wait("bf0", "bf1")
     blocks.share(0, 2)
-    blocks.twins[4].wait_recv()
-    score(1, 1)
+    twins(3, 4)
+    score((1, 0), (1, 1))
     blocks.wait("az2", "bf2", "bf3")
     blocks.share(1, 2)
-    blocks.twins[5].wait_recv()
-    score(1, 3)
-    blocks.twins[6].wait_recv()
-    score(0, 2)
-    blocks.twins[7].wait_recv()
-    score(1, 2)
+    twins(5, 6)
+    score((1, 3), (0, 2))
+    twins(7)
+    score((1, 2))
 
     @pl.loop(0, 16)
     def _(j):
@@ -762,8 +878,8 @@
         out_specs=VMEM,
         scratch_shapes=[
             pltpu.VMEM((16, rows, width), jnp.bfloat16),
-            pltpu.VMEM((2 * rows, hw.shape[1]), jnp.float32),
-            pltpu.VMEM((rows, 128), jnp.float32),
+            pltpu.VMEM((4 * rows, hw.shape[1]), jnp.float32),
+            pltpu.VMEM((3, rows, 128), jnp.float32),
             pltpu.VMEM((16, 8, rows), jnp.float32),
             pltpu.VMEM((16, 8, rows), jnp.float32),
             pltpu.SemaphoreType.DMA((32,)),
@@ -776,10 +892,72 @@
     )(summed, xown, gain, hw, tcol)
 
 
-def attend_kernel(x, w, seg_row, seg_col, out, q, k, vt):
+def attend_kernel(
+    tables,
+    x,
+    w,
+    seg_row,
+    seg_col,
+    first,
+    second,
+    out,
+    new_first,
+    new_second,
+    q,
+    k,
+    vt,
+    packed,
+    got,
+    send_sem,
+    recv_sem,
+    local_sem,
+):
     heads = out.shape[1] // HD
     seq = x.shape[0]
     size = 256
+    me = Place()
+    place = me.dp * 16 + me.fm
+    barrier = pltpu.get_barrier_semaphore()
+
+    @pl.loop(1, 128)
+    def _(t):
+        p = lax.rem(place + t, 128)
+        fm = lax.rem(p, 16)
+        device = (lax.div(p, 16), lax.div(fm, 2), lax.rem(fm, 2))
+        pl.semaphore_signal(barrier, inc=1, device_id=device, device_id_type=MESH)
+
+    @pl.loop(0, 8)
+    def _(i):
+        residue = tables[1, i]
+        for s, source in enumerate((first, second)):
+            for m in range(4):
+                for j in range(3):
+                    packed[i, pl.ds(s * 12 + m * 3 + j, 1)] = source[m, pl.ds(j * 8 + residue, 1)]
+
+    pl.semaphore_wait(barrier, 127)
+
+    def spread(t):
+        p = lax.rem(place + t, 128)
+        dp, fm = lax.div(p, 16), lax.rem(p, 16)
+        return pltpu.make_async_remote_copy(
+            src_ref=packed.at[dp, :, pl.ds(pl.multiple_of(fm * 256, 256), 256)],
+            dst_ref=got.at[place],
+            send_sem=send_sem.at[t],
+            recv_sem=recv_sem.at[t],
+            device_id=(dp, lax.div(fm, 2), lax.rem(fm, 2)),
+            device_id_type=MESH,
+        )
+
+    @pl.loop(1, 128)
+    def _(t):
+        spread(t).start()
+
+    keep = pltpu.make_async_copy(
+        packed.at[me.dp, :, pl.ds(pl.multiple_of(me.fm * 256, 256), 256)],
+        got.at[place],
+        local_sem.at[0],
+    )
+    keep.start()
 
     @pl.loop(0, seq // size)
     def _(i):
@@ -834,54 +1012,49 @@
             _, total, acc = done[h]
             out[rows, pl.ds(h * HD, HD)] = (acc / total).T.astype(out.dtype)
 
-
-def attend(x, w, segments):
+    keep.wait()
+
+    @pl.loop(1, 128)
+    def _(t):
+        spread(t).wait_recv()
+
+    @pl.loop(0, 16)
+    def _(t):
+        holders = [tables[0, t * 8 + u] for u in range(8)]
+        rows = pl.ds(pl.multiple_of(t * 24, 8), 24)
+        for s, target in enumerate((new_first, new_second)):
+            for m in range(4):
+                target[m, rows] = jnp.concatenate(
+                    [got[p, pl.ds(s * 12 + m * 3, 3)] for p in holders], axis=0
+                )
+
+    @pl.loop(1, 128)
+    def _(t):
+        spread(t).wait_send()
+
+
+def attend(tables, x, w, segments, first, second):
     seq = x.shape[0]
     cols = w.shape[2]
+    moment = jax.ShapeDtypeStruct((4, w.shape[1] // 8, cols), first.dtype)
     return pl.pallas_call(
         attend_kernel,
         name="attend",
-        out_shape=jax.ShapeDtypeStruct((seq, cols), x.dtype),
-        in_specs=[VMEM] * 4,
-        out_specs=VMEM,
+        out_shape=(jax.ShapeDtypeStruct((seq, cols), x.dtype), moment, moment),
+        in_specs=[SMEM] + [VMEM] * 6,
+        out_specs=(VMEM,) * 3,
         scratch_shapes=[
             pltpu.VMEM((seq, cols), x.dtype),
             pltpu.VMEM((seq, cols), x.dtype),
             pltpu.VMEM((cols, seq), x.dtype),
+            pltpu.VMEM((8, 24, 16 * cols), first.dtype),
+            pltpu.VMEM((128, 24, cols), first.dtype),
+            pltpu.SemaphoreType.DMA((128,)),
+            pltpu.SemaphoreType.DMA((128,)),
+            pltpu.SemaphoreType.DMA((1,)),
         ],
-        compiler_params=pltpu.CompilerParams(vmem_limit_bytes=60 * 2**20),
-        cost_estimate=pl.CostEstimate(
-            flops=30 * 10**9, bytes_accessed=20 * 2**20, transcendentals=4 * 10**6
-        ),
-    )(x, w, segments[None, :], segments[:, None])
-
-
-def inverse_of(table):
-    total_count = table.shape[0]
-    places = jnp.arange(total_count, dtype=jnp.int32)
-    return jnp.sum(jnp.where(table[None, :] == places[:, None], places[None, :], 0), axis=1)
-
-
-def pack_rows(stored, residues, fm_count):
-    matrices, row_count, columns = stored.shape
-    dp_count = residues.shape[0]
-    split_rows = stored.reshape(
-        matrices, row_count // dp_count, dp_count, fm_count, columns // fm_count
-    )
-    chosen = jnp.take(split_rows, residues, axis=2)
-    return chosen.transpose(2, 3, 0, 1, 4).reshape(
-        dp_count * fm_count, matrices, row_count // dp_count, columns // fm_count
-    )
-
-
-def unpack_rows(received, holder):
-    ordered = jnp.take(received, holder, axis=0)
-    devices, matrices, pair_rows, group_cols = ordered.shape
-    return ordered.transpose(1, 0, 2, 3).reshape(matrices, devices * pair_rows, group_cols)
-
-
-def everywhere(value):
-    return lax.all_to_all(value, ("dp", "fsdp", "mp"), split_axis=0, concat_axis=0, tiled=True)
+        compiler_params=params(3),
+    )(tables, x, w, segments[None, :], segments[:, None], first, second)
 
 
 def body(
@@ -902,42 +1075,25 @@
     group_cols = columns // groups
     model_width = tokens_in.shape[1]
 
-    tables = everywhere(jnp.broadcast_to(jnp.stack([old_block, new_residue], 1), (128, 2)))
-    holder = inverse_of(tables[:, 0])
-    residues = tables[::groups, 1]
-
     by_group = old_weights.reshape(matrices, old_rows, groups, group_cols).transpose(2, 0, 1, 3)
     by_group = by_group.reshape(groups, matrices * old_rows, group_cols)
     small = jnp.stack([segment_ids, target_ids] + [segment_ids] * 6)
-    xfull, sfull, weights = gather_inputs(holder, tokens_in, small, by_group)
-
-    whole_tokens = xfull.reshape(-1, model_width)
+    mark = jnp.where(jnp.arange(8)[:, None] == 0, old_block[0], new_residue[0])
+    mark = jnp.broadcast_to(mark, (8, 128)).astype(jnp.int32)
+    xfull, sfull, weights, tables = gather_inputs(tokens_in, small, mark, by_group)
+
     segments = sfull[:, 0].reshape(-1)
     targets = sfull[:, 1][:, :, None]
     own = me.slot(0, 0)
     xown = lax.dynamic_index_in_dim(xfull, own, 0, keepdims=False)
 
-    first, second, stored, weights = lax.optimization_barrier(
-        (old_first, old_second, old_weights, weights)
+    attended, new_first, new_second = attend(
+        tables, xfull.reshape(-1, model_width), weights, segments, old_first, old_second
     )
-    moments = jnp.concatenate(
-        [pack_rows(first, residues, groups), pack_rows(second, residues, groups)], axis=1
-    )
-    got_moments = everywhere(moments)
-    got_weights = everywhere(pack_rows(stored, residues, groups))
-
-    attended = attend(whole_tokens, weights[:3], segments)
-    attended, got_moments, got_weights = lax.optimization_barrier(
-        (attended, got_moments, got_weights)
-    )
-    summed, heads_used = scatter_parts(
-        attended.reshape(16, -1, group_cols), weights[3], head_weight
+    summed, heads_used, new_weights = scatter_parts(
+        tables, attended.reshape(16, -1, group_cols), weights, head_weight
     )
     loss = finish(summed, xown, norm_gain[None, :], heads_used, targets)[0]
-
-    new_first = unpack_rows(got_moments[:, :matrices], holder)
-    new_second = unpack_rows(got_moments[:, matrices:], holder)
-    new_weights = unpack_rows(got_weights, holder)
     return (new_weights, new_first, new_second, loss)
 
 

time: 377 us -> 316 us (0.84)
  local copies, waits for them, and re-layouts: 47.2 us -> 15 us
  starting transfers between devices: 25 us -> 0 us
  Pallas kernels: 283 us -> 299 us
  waiting for transfers between devices: 10.8 us -> 0 us
  other arithmetic: 8.32 us -> 0.01 us
    all_to_all x3 -> x0, starting transfers between devices: 25 us -> none  [everywhere(): lax.all_to_all(value, ('dp', 'fsdp', 'mp'), split_axis=0, concat_axis=0,...]
    pallas_call x1, Pallas kernels: 46.6 us -> 63.9 us  [attend(): pl.pallas_call(attend_kernel, name='attend', out_shape=(jax.ShapeDtypeStr...]
    gather x6 -> x0, local copies, waits for them, and re-layouts: 15.2 us -> none  [the longest x3 9.05 us: unpack_rows(): ordered = jnp.take(received, holder, axis=0)]
    all_to_all x3 -> x0, waiting for transfers between devices: 10.8 us -> none  [everywhere(): lax.all_to_all(value, ('dp', 'fsdp', 'mp'), split_axis=0, concat_axis=0,...]
    pallas_call x1, Pallas kernels: 87.3 us -> 95.8 us  [gather_inputs(): pl.pallas_call(gather_kernel, name='gather_inputs', out_shape=(jax.ShapeD...]
    slice x4 -> x0, local copies, waits for them, and re-layouts: 7.12 us -> none  [the longest x1 4.8 us: body(): attended = attend(whole_tokens, weights[:3], segments)]
    pallas_call x1, Pallas kernels: 83 us -> 76.1 us  [finish(): pl.pallas_call(finish_kernel, name='finish', out_shape=jax.ShapeDtypeStru...]
    select_n x7 -> x1, other arithmetic: 3.78 us -> 0.01 us  [body(): mark = jnp.where(jnp.arange(8)[:, None] == 0, old_block[0], new_residue[0])]
  transfers between devices with their start and end apart: 3 -> 0, of which waited for: 2 -> 0; matrix products, arithmetic and copies ran while one was open for 5% -> 0% of each run, Pallas kernels for 12% -> 0%
where the time goes in v3:
time: 316 us
  Pallas kernels  299 us (95%)
  local copies, waits for them, and re-layouts  15 us (5%)
    pallas_call x1, Pallas kernels, gather_inputs(): pl.pallas_call(gather_kernel, name='gather_inputs', out_shape=(jax.ShapeD...  95.8 us
    pallas_call x1, Pallas kernels, finish(): pl.pallas_call(finish_kernel, name='finish', out_shape=jax.ShapeDtypeStru...  76.1 us
    pallas_call x1, Pallas kernels, attend(): pl.pallas_call(attend_kernel, name='attend', out_shape=(jax.ShapeDtypeStr...  63.9 us
    pallas_call x1, Pallas kernels, scatter_parts(): pl.pallas_call(scatter_kernel, name='scatter_parts', out_shape=(jax.Shape...  63 us

profile of v3, /device:TPU:1, one launch (start us, length us, event | category | flops | bytes accessed | tf_op | source)
XLA Modules:
  0.0 315.8 jit_solution(5148607673006288851)
XLA Ops:
  0.6 0.0 copy-start.3
  0.6 0.0 copy-start.4
  0.7 2.1 copy.21
  4.1 0.7 broadcast_in_dim.19.mark
  4.8 0.0 copy-done.3
  4.8 0.0 copy-done.4
  4.8 0.6 stack.8.small
  5.4 95.8 %gather_inputs.1 = (bf16[16,128,3072]{2,1,0:T(8,128)(2,1)}, s32[16,8,128]{2,1,0:T(8,128)}, bf16[4,3072,256]{2,1,0:T(8,128)(2,1)}, s32[8,128]{1,0:T(8,128)}) custom-call(bf16[128,3072]{1,0:T(8,128)(2,1)} %tok.1, s32[8,128]{1,0:T(8,128)} %stack.8.small, s32[8,128]{1,0:T(8,128)} %broadcast_in_dim.19.mark, bf16[16,96,256]{2,1,0:T(8,128)(2,1)} %bitcast.26), custom_call_target="tpu_custom_call" | custom-call | tf_op jit(solution)/shard_map/gather_inputs/pallas_call | solution.py:461
  101.2 2.1 dynamic-slice_bitcast_fusion.xown
  103.2 1.5 fusion
  104.8 1.3 copy.17.seg_col
  106.1 63.9 %attend.1 = (bf16[2048,256]{1,0:T(8,128)(2,1)}, f32[4,384,256]{2,1,0:T(8,128)}, f32[4,384,256]{2,1,0:T(8,128)}) custom-call(s32[8,128]{1,0:T(8,128)} %get-tuple-element.14.tables, bf16[2048,3072]{1,0:T(8,128)(2,1)} %bitcast.25, bf16[4,3072,256]{2,1,0:T(8,128)(2,1)} %get-tuple-element.16.w, s32[1,2048]{1,0:T(1,128)} %get-tuple-element.26.seg_row, ...), custom_call_target="tpu_custom_call" | custom-call | tf_op jit(solution)/shard_map/attend/pallas_call | solution.py:1040
  170.0 63.0 %scatter_parts.1 = (f32[128,3072]{1,0:T(8,128)}, bf16[3072,1024]{1,0:T(8,128)(2,1)}, bf16[4,384,256]{2,1,0:T(8,128)(2,1)}) custom-call(s32[8,128]{1,0:T(8,128)} %get-tuple-element.14.tables, bf16[16,128,256]{2,1,0:T(8,128)(2,1)} %bitcast.27, bf16[4,3072,256]{2,1,0:T(8,128)(2,1)} %get-tuple-element.16.w, bf16[3072,1024]{1,0:T(8,128)(2,1)} %hw.1), custom_call_target="tpu_custom_call" | custom-call | tf_op jit(solution)/shard_map/scatter_parts/pallas_call | solution.py:691
  233.0 1.3 copy.18.tcol
  234.4 0.0 copy-start.2
  234.4 76.1 %finish.1 = f32[8,128]{1,0:T(8,128)} custom-call(f32[128,3072]{1,0:T(8,128)} %get-tuple-element.22.summed, bf16[128,3072]{1,0:T(8,128)(2,1)} %dynamic-slice_bitcast_fusion.xown, f32[1,3072]{1,0:T(1,128)} %bitcast.37, bf16[3072,1024]{1,0:T(8,128)(2,1)} %get-tuple-element.23.hw, s32[16,128,1]{2,1,0:T(8,128)} %copy.18.tcol), custom_call_target="tpu_custom_call" | custom-call | tf_op jit(solution)/shard_map/finish/pallas_call | solution.py:873
  310.5 0.0 copy-start.1
  310.5 1.3 slice_bitcast_fusion.2
  311.8 0.0 copy-done.2
  311.8 0.9 copy.27
  312.7 0.0 copy-done.1
  312.7 0.0 copy-start
  312.7 1.1 copy.28
  313.8 0.8 copy-done
  314.6 1.1 copy.29
  (1 shorter events, 0.0 us)
Async XLA Ops:
  0.6 4.1 %copy-start.3 = (s32[128]{0:T(128)S(1)}, s32[128]{0:T(128)}, u32[]{:S(2)}) copy-start(s32[128]{0:T(128)} %param.11) | copy-start | bytes 1540
  0.6 4.1 %copy-start.4 = (s32[128]{0:T(128)S(1)}, s32[128]{0:T(128)}, u32[]{:S(2)}) copy-start(s32[128]{0:T(128)} %param.12) | copy-start | bytes 1540
  234.4 77.4 %copy-start.2 = (bf16[4,384,256]{2,1,0:T(8,128)(2,1)S(1)}, bf16[4,384,256]{2,1,0:T(8,128)(2,1)}, u32[]{:S(2)}) copy-start(bf16[4,384,256]{2,1,0:T(8,128)(2,1)} %get-tuple-element.31) | copy-start | bytes 2359300
  310.5 2.2 copy-start.1
  312.7 2.0 copy-start

commit v4 on v3

--- a/solution.py
+++ b/solution.py
@@ -161,9 +161,11 @@
         self.share(1, 1)
         self.share(1, 3)
 
-    def last(self):
+    def fifth(self):
         self.wait("bf0", "bf1")
         self.share(0, 2)
+
+    def last(self):
         self.wait("az2", "bf2", "bf3")
         self.share(1, 2)
         for copy in self.twins:
@@ -174,12 +176,22 @@
     tok,
     small,
     mark,
-    wpk,
-    xfull,
+    stored,
+    first,
+    second,
+    xown,
     sfull,
     wlog,
     tables,
-    wfull,
+    q,
+    k,
+    vt,
+    moments,
+    xfull,
+    wq,
+    wk,
+    wv,
+    wo,
     wown,
     marks,
     holder,
@@ -192,6 +204,8 @@
     small_recv,
     mark_send,
     mark_recv,
+    mom_send,
+    mom_recv,
 ):
     me = Place()
     sends = Sends(send_sem, recv_sem)
@@ -203,6 +217,11 @@
             for core in (0, 1)
         ],
     )
+    width = wlog.shape[2]
+    wfull = (wq, wk, wv, wo)
+
+    def columns(t):
+        return pl.ds(pl.multiple_of(t * width, width), width)
 
     keep = pltpu.make_async_copy(tok, xfull.at[me.fm], local_sem.at[0])
     swap = sends.make(tok, xfull.at[me.fm], me.across(1 - me.c))
@@ -215,67 +234,80 @@
     def _():
         swap.start()
 
-    def exchange(k):
-        t = lax.rem(me.fm + k, 16)
-        return pltpu.make_async_remote_copy(
-            src_ref=wpk.at[t],
-            dst_ref=wown.at[me.fm],
-            send_sem=ex_send.at[k],
-            recv_sem=ex_recv.at[k],
-            device_id=(me.dp, lax.div(t, 2), lax.rem(t, 2)),
-            device_id_type=MESH,
-        )
-
     place = me.dp * 16 + me.fm
 
-    def mark_plane(k):
-        t = lax.rem(me.fm + k, 16)
+    def mark_plane(j):
+        t = lax.rem(me.fm + j, 16)
         return pltpu.make_async_remote_copy(
             src_ref=mark,
             dst_ref=marks.at[place],
-            send_sem=mark_send.at[k],
-            recv_sem=mark_recv.at[k],
+            send_sem=mark_send.at[j],
+            recv_sem=mark_recv.at[j],
             device_id=(me.dp, lax.div(t, 2), lax.rem(t, 2)),
             device_id_type=MESH,
         )
 
-    def mark_rest(k):
+    def mark_rest(j):
         plane = marks.at[pl.ds(me.dp * 16, 16)]
         return pltpu.make_async_remote_copy(
             src_ref=plane,
             dst_ref=plane,
-            send_sem=mark_send.at[16 + k],
-            recv_sem=mark_recv.at[16 + k],
-            device_id=(lax.rem(me.dp + k, 8), me.fs, me.g),
+            send_sem=mark_send.at[16 + j],
+            recv_sem=mark_recv.at[16 + j],
+            device_id=(lax.rem(me.dp + j, 8), me.fs, me.g),
             device_id_type=MESH,
         )
 
-    mark_own = pltpu.make_async_copy(mark, marks.at[place], local_sem.at[4])
+    def exchange(j):
+        t = lax.rem(me.fm + j, 16)
+        return pltpu.make_async_remote_copy(
+            src_ref=stored.at[:, :, columns(t)],
+            dst_ref=wown.at[:, me.fm],
+            send_sem=ex_send.at[j],
+            recv_sem=ex_recv.at[j],
+            device_id=(me.dp, lax.div(t, 2), lax.rem(t, 2)),
+            device_id_type=MESH,
+        )
+
+    def move_moments(j, which):
+        t = lax.rem(me.fm + j, 16)
+        return pltpu.make_async_remote_copy(
+            src_ref=(first, second)[which].at[:, :, columns(t)],
+            dst_ref=moments.at[me.fm, pl.ds(which * 4, 4)],
+            send_sem=mom_send.at[which * 16 + j],
+            recv_sem=mom_recv.at[which * 16 + j],
+            device_id=(me.dp, lax.div(t, 2), lax.rem(t, 2)),
+            device_id_type=MESH,
+        )
+
+    mark_own = pltpu.make_async_copy(mark, marks.at[place], local_sem.at[1])
     mark_own.start()
 
     @pl.loop(1, 16)
-    def _(k):
-        mark_plane(k).start()
+    def _(j):
+        mark_plane(j).start()
 
     @pl.loop(1, 16)
-    def _(k):
-        exchange(k).start()
-
-    own = pltpu.make_async_copy(wpk.at[me.fm], wown.at[me.fm], local_sem.at[1])
+    def _(j):
+        exchange(j).start()
+
+    own = pltpu.make_async_copy(
+        stored.at[:, :, columns(me.fm)], wown.at[:, me.fm], local_sem.at[2]
+    )
     own.start()
 
-    def tell(k):
-        q = lax.rem(me.c * 8 + me.fs + k, 16)
+    def tell(j):
+        p = lax.rem(me.c * 8 + me.fs + j, 16)
         return pltpu.make_async_remote_copy(
             src_ref=small,
             dst_ref=sfull.at[me.fm],
-            send_sem=small_send.at[k],
+            send_sem=small_send.at[j],
             recv_sem=small_recv.at[me.fm],
-            device_id=(me.x * 2 + lax.div(q, 8), lax.rem(q, 8), me.c),
+            device_id=(me.x * 2 + lax.div(p, 8), lax.rem(p, 8), me.c),
             device_id_type=MESH,
         )
 
-    note = pltpu.make_async_copy(small, sfull.at[me.fm], local_sem.at[2])
+    note = pltpu.make_async_copy(small, sfull.at[me.fm], local_sem.at[3])
 
     @pl.when(me.n == 1)
     def _():
@@ -286,8 +318,8 @@
         note.start()
 
     @pl.loop(1, 16)
-    def _(k):
-        tell(k).start()
+    def _(j):
+        tell(j).start()
 
     @pl.when(me.n == 0)
     def _():
@@ -299,80 +331,104 @@
 
     blocks = BlockGather(me, xfull, sends)
     blocks.first()
+    hold = pltpu.make_async_copy(xfull.at[me.slot(0, 0)], xown, local_sem.at[4])
+    hold.start()
 
     mark_own.wait()
 
     @pl.loop(1, 16)
-    def _(k):
-        mark_plane(k).wait_recv()
+    def _(j):
+        mark_plane(j).wait_recv()
 
     @pl.loop(1, 8)
-    def _(k):
-        mark_rest(k).start()
+    def _(j):
+        mark_rest(j).start()
 
     own.wait()
 
     @pl.loop(1, 16)
-    def _(k):
-        exchange(k).wait_recv()
-
-    far = pltpu.make_async_remote_copy(
-        src_ref=wown,
-        dst_ref=wfull.at[pl.ds(me.dp * 16, 16)],
-        send_sem=ex_send.at[16],
-        recv_sem=ex_recv.at[16 + me.c],
-        device_id=me.across(me.g),
-        device_id_type=MESH,
-    )
-    far.start()
-    near = pltpu.make_async_remote_copy(
-        src_ref=wown,
-        dst_ref=wfull.at[pl.ds(me.dp * 16, 16)],
-        send_sem=ex_send.at[17],
-        recv_sem=ex_recv.at[18],
-        device_id=me.twin(),
-        device_id_type=MESH,
-    )
-    stay = pltpu.make_async_copy(wown, wfull.at[pl.ds(me.dp * 16, 16)], local_sem.at[3])
-
-    @pl.when(me.n == 1)
-    def _():
-        near.start()
-
-    @pl.when(me.n == 0)
-    def _():
-        stay.start()
-
-    blocks.second()
-
-    def from_core(core):
+    def _(j):
+        exchange(j).wait_recv()
+
+    def far(m, core):
         return pltpu.make_async_remote_copy(
-            src_ref=wown,
-            dst_ref=wfull.at[pl.ds(me.dp * 16, 16)],
-            send_sem=ex_send.at[16],
-            recv_sem=ex_recv.at[16 + core],
+            src_ref=wown.at[m],
+            dst_ref=wfull[m].at[pl.ds(me.dp * 16, 16)],
+            send_sem=ex_send.at[16 + m],
+            recv_sem=ex_recv.at[16 + m * 2 + core],
             device_id=me.across(me.g),
             device_id_type=MESH,
         )
 
-    @pl.when(me.n == 1)
-    def _():
-        from_core(0).wait_recv()
-        from_core(1).wait_recv()
-
-    @pl.when(me.n == 0)
-    def _():
-        near.wait_recv()
-        stay.wait()
+    def near(m):
+        return pltpu.make_async_remote_copy(
+            src_ref=wown.at[m],
+            dst_ref=wfull[m].at[pl.ds(me.dp * 16, 16)],
+            send_sem=ex_send.at[20 + m],
+            recv_sem=ex_recv.at[24 + m],
+            device_id=me.twin(),
+            device_id_type=MESH,
+        )
+
+    def stay(m):
+        return pltpu.make_async_copy(
+            wown.at[m], wfull[m].at[pl.ds(me.dp * 16, 16)], local_sem.at[6 + m]
+        )
+
+    for m in range(4):
+        far(m, me.c).start()
+
+        @pl.when(me.n == 1)
+        def _():
+            near(m).start()
+
+        @pl.when(me.n == 0)
+        def _():
+            stay(m).start()
 
     right, left = me.at(rx=1), me.at(rx=3)
-    pair = wfull.at[pl.ds(me.x * 32, 32)]
-    to_right = sends.start(pair, pair, right)
-    to_left = sends.start(pair, pair, left)
+    ring = {}
+
+    def both_ways(m):
+        @pl.when(me.n == 1)
+        def _():
+            far(m, 0).wait_recv()
+            far(m, 1).wait_recv()
+
+        @pl.when(me.n == 0)
+        def _():
+            near(m).wait_recv()
+            stay(m).wait()
+
+        pair = wfull[m].at[pl.ds(me.x * 32, 32)]
+        ring[m] = [sends.start(pair, pair, right), sends.start(pair, pair, left)]
+
+    def pass_on(m):
+        ring[m][0].wait_recv()
+        one = wfull[m].at[pl.ds(lax.rem(me.x + 3, 4) * 32, 16)]
+        on_right = sends.start(one, one, right)
+        ring[m][1].wait_recv()
+        two = wfull[m].at[pl.ds(lax.rem(me.x + 1, 4) * 32 + 16, 16)]
+        on_left = sends.start(two, two, left)
+        ring[m] = [on_right, on_left]
+
+    rows = stored.shape[1]
+
+    def in_order(m):
+        for copy in ring[m]:
+            copy.wait_recv()
+
+        @pl.loop(0, 128)
+        def _(b):
+            wlog[m, pl.ds(pl.multiple_of(b * rows, 8), rows)] = wfull[m][holder[0, b]]
+
+    blocks.second()
+    for m in range(3):
+        both_ways(m)
 
     @pl.loop(1, 8)
-    def _(k):
-        mark_rest(k).wait_recv()
+    def _(j):
+        mark_rest(j).wait_recv()
 
     lane = lax.broadcasted_iota(jnp.int32, (8, 128), 1)
     line = lax.broadcasted_iota(jnp.int32, (8, 128), 0)
@@ -388,28 +444,58 @@
     tables[...] = jnp.where(line == 0, jnp.minimum(found, 127), residues)
     tell_scalar = pltpu.make_async_copy(tables, holder, local_sem.at[5])
     tell_scalar.start()
+
     blocks.third()
+    pass_on(0)
     blocks.fourth()
-    to_right.wait_recv()
-    first = wfull.at[pl.ds(lax.rem(me.x + 3, 4) * 32, 16)]
-    on_right = sends.start(first, first, right)
-    to_left.wait_recv()
-    second = wfull.at[pl.ds(lax.rem(me.x + 1, 4) * 32 + 16, 16)]
-    on_left = sends.start(second, second, left)
+    pass_on(1)
+    blocks.fifth()
+
+    @pl.loop(1, 16)
+    def _(j):
+        for which in (0, 1):
+            move_moments(j, which).start()
+
+    keep_moments = [
+        pltpu.make_async_copy(
+            source.at[:, :, columns(me.fm)],
+            moments.at[me.fm, pl.ds(which * 4, 4)],
+            local_sem.at[10 + which],
+        )
+        for which, source in enumerate((first, second))
+    ]
+    for copy in keep_moments:
+        copy.start()
+
+    pass_on(2)
+    both_ways(3)
     blocks.last()
-    on_right.wait_recv()
-    on_left.wait_recv()
-
-    rows = wpk.shape[1] // 4
     tell_scalar.wait()
 
-    @pl.loop(0, 128)
-    def _(b):
-        where = holder[0, b]
-        for m in range(4):
-            wlog[m, pl.ds(pl.multiple_of(b * rows, 8), rows)] = wfull[
-                where, pl.ds(m * rows, rows)
-            ]
+    def project(m, write):
+        @pl.loop(0, 4)
+        def _(i):
+            block = xfull[pl.ds(i * 4, 4)].reshape(512, xfull.shape[2])
+            value = jnp.dot(block, wlog[m], preferred_element_type=jnp.float32)
+            write(pl.ds(pl.multiple_of(i * 512, 512), 512), value.astype(q.dtype))
+
+    def write_q(part, value):
+        q[part] = value
+
+    def write_k(part, value):
+        k[part] = value
+
+    def write_v(part, value):
+        vt[:, part] = value.T
+
+    in_order(0)
+    project(0, write_q)
+    in_order(1)
+    project(1, write_k)
+    in_order(2)
+    project(2, write_v)
+    pass_on(3)
+    in_order(3)
 
     @pl.loop(0, 16)
     def _(j):
@@ -425,27 +511,40 @@
             ).wait_recv()
 
     @pl.loop(1, 16)
-    def _(k):
-        exchange(k).wait_send()
-        tell(k).wait_send()
-        mark_plane(k).wait_send()
+    def _(j):
+        for which in (0, 1):
+            move_moments(j, which).wait_recv()
+
+    for copy in keep_moments:
+        copy.wait()
+
+    @pl.loop(1, 16)
+    def _(j):
+        exchange(j).wait_send()
+        tell(j).wait_send()
+        mark_plane(j).wait_send()
+        for which in (0, 1):
+            move_moments(j, which).wait_send()
 
     @pl.loop(1, 8)
-    def _(k):
-        mark_rest(k).wait_send()
-
-    far.wait_send()
+    def _(j):
+        mark_rest(j).wait_send()
+
+    for m in range(4):
+        far(m, me.c).wait_send()
 
     @pl.when(me.n == 1)
     def _():
         tell(0).wait_send()
-        near.wait_send()
         swap.wait_send()
+        for m in range(4):
+            near(m).wait_send()
 
     @pl.when(me.n == 0)
     def _():
         note.wait()
 
+    hold.wait()
     sends.finish()
 
 
@@ -455,37 +554,49 @@
     )
 
 
-def gather_inputs(tokens, small, mark, wpk):
+def gather_inputs(tokens, small, mark, stored, first, second):
     rows, width = tokens.shape
-    old_rows = wpk.shape[1] // 4
+    matrices, old_rows, columns = stored.shape
+    cols = columns // 16
+    dtype = tokens.dtype
     return pl.pallas_call(
         gather_kernel,
         name="gather_inputs",
         out_shape=(
-            jax.ShapeDtypeStruct((16, rows, width), tokens.dtype),
+            jax.ShapeDtypeStruct((rows, width), dtype),
             jax.ShapeDtypeStruct((16, *small.shape), small.dtype),
-            jax.ShapeDtypeStruct((4, 128 * old_rows, wpk.shape[2]), wpk.dtype),
+            jax.ShapeDtypeStruct((matrices, width, cols), dtype),
             jax.ShapeDtypeStruct((8, 128), jnp.int32),
+            jax.ShapeDtypeStruct((16 * rows, cols), dtype),
+            jax.ShapeDtypeStruct((16 * rows, cols), dtype),
+            jax.ShapeDtypeStruct((cols, 16 * rows), dtype),
+            jax.ShapeDtypeStruct((16, 2 * matrices, old_rows, cols), first.dtype),
         ),
-        in_specs=[VMEM] * 4,
-        out_specs=(ANY, VMEM, VMEM, VMEM),
+        in_specs=[VMEM] * 4 + [ANY] * 2,
+        out_specs=(ANY,) + (VMEM,) * 6 + (ANY,),
         scratch_shapes=[
-            pltpu.VMEM((128, *wpk.shape[1:]), wpk.dtype),
-            pltpu.VMEM(wpk.shape, wpk.dtype),
+            pltpu.VMEM((16, rows, width), dtype),
+            pltpu.VMEM((128, old_rows, cols), dtype),
+            pltpu.VMEM((128, old_rows, cols), dtype),
+            pltpu.VMEM((128, old_rows, cols), dtype),
+            pltpu.VMEM((128, old_rows, cols), dtype),
+            pltpu.VMEM((matrices, 16, old_rows, cols), dtype),
             pltpu.VMEM((128, 8, 128), jnp.int32),
             pltpu.SMEM((8, 128), jnp.int32),
-            pltpu.SemaphoreType.DMA((40,)),
-            pltpu.SemaphoreType.DMA((40,)),
-            pltpu.SemaphoreType.DMA((6,)),
-            pltpu.SemaphoreType.DMA((18,)),
-            pltpu.SemaphoreType.DMA((19,)),
+            pltpu.SemaphoreType.DMA((48,)),
+            pltpu.SemaphoreType.DMA((48,)),
+            pltpu.SemaphoreType.DMA((12,)),
+            pltpu.SemaphoreType.DMA((24,)),
+            pltpu.SemaphoreType.DMA((28,)),
             pltpu.SemaphoreType.DMA((16,)),
             pltpu.SemaphoreType.DMA((16,)),
             pltpu.SemaphoreType.DMA((24,)),
             pltpu.SemaphoreType.DMA((24,)),
+            pltpu.SemaphoreType.DMA((32,)),
+            pltpu.SemaphoreType.DMA((32,)),
         ],
         compiler_params=params(0),
-    )(tokens, small, mark, wpk)
+    )(tokens, small, mark, stored, first, second)
 
 
 def add_rows(into, start, end, *others):
@@ -499,12 +610,18 @@
 
 
 def scatter_kernel(
-    tables, att, w, hw, out, hwx, nw, tw, parts, r, za, zb, fa0, fa1, ya, fb0, fb1, yb, send_sem, recv_sem, local_sem, hs, hr
+    tables, att, w_all, hw, out, hwx, nw, w, tw, parts, r, za, zb, fa0, fa1, ya, fb0, fb1, yb, send_sem, recv_sem, local_sem, hs, hr
 ):
     me = Place()
     sends = Sends(send_sem, recv_sem)
     up, down, over, twin = me.at(ry=1), me.at(ry=3), me.at(rz=1), me.twin()
     right, left, partner = me.at(rx=1), me.at(rx=3), me.across(me.c)
+    fetch = [
+        pltpu.make_async_copy(w_all.at[part], w.at[part], local_sem.at[j])
+        for j, part in enumerate((pl.ds(3, 1), pl.ds(0, 3)))
+    ]
+    for copy in fetch:
+        copy.start()
     greet([up, down, over, twin, right, left, partner])
 
     order = [(1, 2), (1, 0), (1, 1), (1, 3), (0, 2), (0, 1), (0, 3), (0, 0)]
@@ -523,7 +640,6 @@
         )
 
     head_out = head_copy(0, me.x * quarter, quarter, partner, hw)
-    head_keep = pltpu.make_async_copy(hw, hwx, local_sem.at[0])
     head_right = head_copy(1, me.x * quarter, quarter, right, hwx)
     head_left = head_copy(2, me.x * quarter, quarter, left, hwx)
     head_right2 = head_copy(3, lax.rem(me.x + 3, 4) * quarter, half, right, hwx)
@@ -532,7 +648,6 @@
     @pl.when(me.n == 0)
     def _():
         head_out.start()
-        head_keep.start()
 
     def project(slot, write):
         @pl.loop(0, out.shape[1] // 512)
@@ -567,6 +682,7 @@
         project(me.slot(rz, ry), write)
 
     a_got, b_got, y_got = {}, {}, {}
+    fetch[0].wait()
     halves = [halve(*order[0]), halve(*order[1])]
     for at, (rz, ry) in enumerate(order):
         if at + 2 < 8:
@@ -587,6 +703,7 @@
         head_left.start()
 
     give = sends.make(tw, nw, twin)
+    fetch[1].wait()
 
     @pl.when(me.n == 0)
     def _():
@@ -679,7 +796,6 @@
     def _():
         give.wait_send()
         head_out.wait_send()
-        head_keep.wait()
 
     sends.finish()
 
@@ -696,9 +812,10 @@
             jax.ShapeDtypeStruct(hw.shape, hw.dtype),
             jax.ShapeDtypeStruct(kept, w.dtype),
         ),
-        in_specs=[SMEM] + [VMEM] * 3,
+        in_specs=[SMEM, VMEM, ANY, ANY],
         out_specs=(VMEM, ANY, VMEM),
         scratch_shapes=[
+            pltpu.VMEM(w.shape, w.dtype),
             pltpu.VMEM(kept, w.dtype),
             pltpu.VMEM((8, rows, width), dtype),
             pltpu.VMEM((8, rows, width), dtype),
@@ -712,7 +829,7 @@
             pltpu.VMEM((4, rows - A_END, width), dtype),
             pltpu.SemaphoreType.DMA((32,)),
             pltpu.SemaphoreType.DMA((32,)),
-            pltpu.SemaphoreType.DMA((1,)),
+            pltpu.SemaphoreType.DMA((2,)),
             pltpu.SemaphoreType.DMA((5,)),
             pltpu.SemaphoreType.DMA((5,)),
         ],
@@ -721,12 +838,21 @@
 
 
 def finish_kernel(
+    tables,
     summed,
     xown,
     gain,
+    tcol,
+    hw_own,
+    hw_far,
+    moments_all,
+    loss,
+    new_first,
+    new_second,
     hw,
-    tcol,
-    loss,
+    moments,
+    packed,
+    got_moments,
     full,
     lg,
     cols,
@@ -740,7 +866,28 @@
 ):
     me = Place()
     sends = Sends(send_sem, recv_sem)
-    greet_plane(me)
+
+    def fetch_head(source):
+        return pltpu.make_async_copy(source, hw, local_sem.at[1])
+
+    @pl.when(me.n == 0)
+    def _():
+        fetch_head(hw_own).start()
+
+    @pl.when(me.n == 1)
+    def _():
+        fetch_head(hw_far).start()
+
+    fetch_moments = pltpu.make_async_copy(moments_all, moments, local_sem.at[2])
+    fetch_moments.start()
+    greet_plane(
+        me,
+        [
+            (lax.rem(me.x + rx, 4) * 2 + core, me.fs, me.g)
+            for rx in (1, 2, 3)
+            for core in (0, 1)
+        ],
+    )
     own = me.slot(0, 0)
     width = summed.shape[1]
 
@@ -814,7 +961,41 @@
         for k in which:
             blocks.twins[k].wait_recv()
 
+    mine = pl.ds(me.dp * 16, 16)
+
+    def to_dp(j):
+        dp = lax.rem(me.dp + j, 8)
+        return pltpu.make_async_remote_copy(
+            src_ref=packed.at[dp],
+            dst_ref=got_moments.at[mine],
+            send_sem=send_sem.at[32 + j],
+            recv_sem=recv_sem.at[32 + j],
+            device_id=(dp, me.fs, me.g),
+            device_id_type=MESH,
+        )
+
+    keep_moments = pltpu.make_async_copy(
+        packed.at[me.dp], got_moments.at[mine], local_sem.at[3]
+    )
+
     blocks.first()
+
+    fetch_moments.wait()
+
+    @pl.loop(0, 16)
+    def _(p):
+        for i in range(8):
+            residue = tables[1, i]
+            for m in range(8):
+                for j in range(3):
+                    packed[i, p, pl.ds(m * 3 + j, 1)] = moments[p, m, pl.ds(j * 8 + residue, 1)]
+
+    @pl.loop(1, 8)
+    def _(j):
+        to_dp(j).start()
+
+    keep_moments.start()
+    fetch_head(hw_own).wait()
     twins(0)
     score((0, 0))
     blocks.second()
@@ -822,12 +1003,28 @@
     twins(1, 2)
     score((0, 1), (0, 3))
     blocks.fourth()
-    blocks.wait("bf0", "bf1")
-    blocks.share(0, 2)
+    blocks.fifth()
     twins(3, 4)
     score((1, 0), (1, 1))
     blocks.wait("az2", "bf2", "bf3")
     blocks.share(1, 2)
+
+    keep_moments.wait()
+
+    @pl.loop(1, 8)
+    def _(j):
+        to_dp(j).wait_recv()
+
+    @pl.loop(0, 16)
+    def _(t):
+        holders = [tables[0, t * 8 + u] for u in range(8)]
+        rows = pl.ds(pl.multiple_of(t * 24, 8), 24)
+        for s, target in enumerate((new_first, new_second)):
+            for m in range(4):
+                target[m, rows] = jnp.concatenate(
+                    [got_moments[p, pl.ds(s * 12 + m * 3, 3)] for p in holders], axis=0
+                )
+
     twins(5, 6)
     score((1, 3), (0, 2))
     twins(7)
@@ -865,118 +1062,57 @@
         def _():
             tell(b).wait_send()
 
+    @pl.loop(1, 8)
+    def _(j):
+        to_dp(j).wait_send()
+
     sends.finish()
 
 
-def finish(summed, xown, gain, hw, tcol):
+def finish(tables, summed, xown, gain, tcol, hw_own, hw_far, moments):
     rows, width = summed.shape
+    holders, sets, old_rows, cols = moments.shape
+    dtype = moments.dtype
+    kept = jax.ShapeDtypeStruct((sets // 2, width // 8, cols), dtype)
     return pl.pallas_call(
         finish_kernel,
         name="finish",
-        out_shape=jax.ShapeDtypeStruct((8, rows), jnp.float32),
-        in_specs=[VMEM] * 5,
-        out_specs=VMEM,
+        out_shape=(jax.ShapeDtypeStruct((8, rows), jnp.float32), kept, kept),
+        in_specs=[SMEM] + [VMEM] * 4 + [ANY] * 3,
+        out_specs=(VMEM,) * 3,
         scratch_shapes=[
+            pltpu.VMEM(hw_own.shape, hw_own.dtype),
+            pltpu.VMEM(moments.shape, dtype),
+            pltpu.VMEM((8, holders, sets * 3, cols), dtype),
+            pltpu.VMEM((8 * holders, sets * 3, cols), dtype),
             pltpu.VMEM((16, rows, width), jnp.bfloat16),
-            pltpu.VMEM((4 * rows, hw.shape[1]), jnp.float32),
+            pltpu.VMEM((4 * rows, hw_own.shape[1]), jnp.float32),
             pltpu.VMEM((3, rows, 128), jnp.float32),
             pltpu.VMEM((16, 8, rows), jnp.float32),
             pltpu.VMEM((16, 8, rows), jnp.float32),
-            pltpu.SemaphoreType.DMA((32,)),
-            pltpu.SemaphoreType.DMA((32,)),
-            pltpu.SemaphoreType.DMA((1,)),
+            pltpu.SemaphoreType.DMA((40,)),
+            pltpu.SemaphoreType.DMA((40,)),
+            pltpu.SemaphoreType.DMA((4,)),
             pltpu.SemaphoreType.DMA((16,)),
             pltpu.SemaphoreType.DMA((16,)),
         ],
         compiler_params=params(1),
-    )(summed, xown, gain, hw, tcol)
-
-
-def attend_kernel(
-    tables,
-    x,
-    w,
-    seg_row,
-    seg_col,
-    first,
-    second,
-    out,
-    new_first,
-    new_second,
-    q,
-    k,
-    vt,
-    packed,
-    got,
-    send_sem,
-    recv_sem,
-    local_sem,
-):
+    )(tables, summed, xown, gain, tcol, hw_own, hw_far, moments)
+
+
+def attend_kernel(begin, q, k, vt, seg_row, seg_col, out):
     heads = out.shape[1] // HD
-    seq = x.shape[0]
+    seq = q.shape[0]
     size = 256
-    me = Place()
-    place = me.dp * 16 + me.fm
-    barrier = pltpu.get_barrier_semaphore()
-
-    @pl.loop(1, 128)
-    def _(t):
-        p = lax.rem(place + t, 128)
-        fm = lax.rem(p, 16)
-        device = (lax.div(p, 16), lax.div(fm, 2), lax.rem(fm, 2))
-        pl.semaphore_signal(barrier, inc=1, device_id=device, device_id_type=MESH)
-
-    @pl.loop(0, 8)
-    def _(i):
-        residue = tables[1, i]
-        for s, source in enumerate((first, second)):
-            for m in range(4):
-                for j in range(3):
-                    packed[i, pl.ds(s * 12 + m * 3 + j, 1)] = source[m, pl.ds(j * 8 + residue, 1)]
-
-    pl.semaphore_wait(barrier, 127)
-
-    def spread(t):
-        p = lax.rem(place + t, 128)
-        dp, fm = lax.div(p, 16), lax.rem(p, 16)
-        return pltpu.make_async_remote_copy(
-            src_ref=packed.at[dp, :, pl.ds(pl.multiple_of(fm * 256, 256), 256)],
-            dst_ref=got.at[place],
-            send_sem=send_sem.at[t],
-            recv_sem=recv_sem.at[t],
-            device_id=(dp, lax.div(fm, 2), lax.rem(fm, 2)),
-            device_id_type=MESH,
-        )
-
-    @pl.loop(1, 128)
-    def _(t):
-        spread(t).start()
-
-    keep = pltpu.make_async_copy(
-        packed.at[me.dp, :, pl.ds(pl.multiple_of(me.fm * 256, 256), 256)],
-        got.at[place],
-        local_sem.at[0],
+    scale = math.log2(math.e) / math.sqrt(HD)
+    ahead = lax.broadcasted_iota(jnp.int32, (size, size), 0) - lax.broadcasted_iota(
+        jnp.int32, (size, size), 1
     )
-    keep.start()
-
-    @pl.loop(0, seq // size)
-    def _(i):
-        rows = pl.ds(pl.multiple_of(i * size, size), size)
-        block = x[rows]
-        q[rows] = jnp.dot(block, w[0], preferred_element_type=jnp.float32).astype(q.dtype)
-        k[rows] = jnp.dot(block, w[1], preferred_element_type=jnp.float32).astype(k.dtype)
-        v = jnp.dot(block, w[2], preferred_element_type=jnp.float32)
-        vt[:, rows] = v.T.astype(vt.dtype)
-
-    scale = math.log2(math.e) / math.sqrt(HD)
 
     @pl.loop(0, seq // size)
     def _(i):
         rows = pl.ds(pl.multiple_of(i * size, size), size)
         own = seg_row[0:1, rows]
-        ahead = lax.broadcasted_iota(jnp.int32, (size, size), 0) - lax.broadcasted_iota(
-            jnp.int32, (size, size), 1
-        )
 
         def step(j, carry):
             cols = pl.ds(pl.multiple_of(j * size, size), size)
@@ -1007,54 +1143,24 @@
             jnp.zeros((1, size), jnp.float32),
             jnp.zeros((HD, size), jnp.float32),
         )
-        done = lax.fori_loop(0, i + 1, step, (start,) * heads)
+        done = lax.fori_loop(begin[i], i + 1, step, (start,) * heads)
         for h in range(heads):
             _, total, acc = done[h]
             out[rows, pl.ds(h * HD, HD)] = (acc / total).T.astype(out.dtype)
 
-    keep.wait()
-
-    @pl.loop(1, 128)
-    def _(t):
-        spread(t).wait_recv()
-
-    @pl.loop(0, 16)
-    def _(t):
-        holders = [tables[0, t * 8 + u] for u in range(8)]
-        rows = pl.ds(pl.multiple_of(t * 24, 8), 24)
-        for s, target in enumerate((new_first, new_second)):
-            for m in range(4):
-                target[m, rows] = jnp.concatenate(
-                    [got[p, pl.ds(s * 12 + m * 3, 3)] for p in holders], axis=0
-                )
-
-    @pl.loop(1, 128)
-    def _(t):
-        spread(t).wait_send()
-
-
-def attend(tables, x, w, segments, first, second):
-    seq = x.shape[0]
-    cols = w.shape[2]
-    moment = jax.ShapeDtypeStruct((4, w.shape[1] // 8, cols), first.dtype)
+
+def attend(q, k, vt, segments):
+    seq = q.shape[0]
+    heads_of = segments.reshape(-1, 256)[:, :1]
+    begin = jnp.sum((segments[None, :] < heads_of).astype(jnp.int32), axis=1) // 256
     return pl.pallas_call(
         attend_kernel,
         name="attend",
-        out_shape=(jax.ShapeDtypeStruct((seq, cols), x.dtype), moment, moment),
-        in_specs=[SMEM] + [VMEM] * 6,
-        out_specs=(VMEM,) * 3,
-        scratch_shapes=[
-            pltpu.VMEM((seq, cols), x.dtype),
-            pltpu.VMEM((seq, cols), x.dtype),
-            pltpu.VMEM((cols, seq), x.dtype),
-            pltpu.VMEM((8, 24, 16 * cols), first.dtype),
-            pltpu.VMEM((128, 24, cols), first.dtype),
-            pltpu.SemaphoreType.DMA((128,)),
-            pltpu.SemaphoreType.DMA((128,)),
-            pltpu.SemaphoreType.DMA((1,)),
-        ],
-        compiler_params=params(3),
-    )(tables, x, w, segments[None, :], segments[:, None], first, second)
+        out_shape=jax.ShapeDtypeStruct(q.shape, q.dtype),
+        in_specs=[SMEM] + [VMEM] * 5,
+        out_specs=VMEM,
+        compiler_params=pltpu.CompilerParams(vmem_limit_bytes=60 * 2**20),
+    )(begin, q, k, vt, segments[None, :], segments[:, None])
 
 
 def body(
@@ -1069,32 +1175,22 @@
     norm_gain,
     head_weight,
 ):
-    me = Place()
-    matrices, old_rows, columns = old_weights.shape
-    groups = 16
-    group_cols = columns // groups
-    model_width = tokens_in.shape[1]
-
-    by_group = old_weights.reshape(matrices, old_rows, groups, group_cols).transpose(2, 0, 1, 3)
-    by_group = by_group.reshape(groups, matrices * old_rows, group_cols)
     small = jnp.stack([segment_ids, target_ids] + [segment_ids] * 6)
     mark = jnp.where(jnp.arange(8)[:, None] == 0, old_block[0], new_residue[0])
     mark = jnp.broadcast_to(mark, (8, 128)).astype(jnp.int32)
-    xfull, sfull, weights, tables = gather_inputs(tokens_in, small, mark, by_group)
-
+    xown, sfull, weights, tables, q, k, vt, moments = gather_inputs(
+        tokens_in, small, mark, old_weights, old_first, old_second
+    )
     segments = sfull[:, 0].reshape(-1)
     targets = sfull[:, 1][:, :, None]
-    own = me.slot(0, 0)
-    xown = lax.dynamic_index_in_dim(xfull, own, 0, keepdims=False)
-
-    attended, new_first, new_second = attend(
-        tables, xfull.reshape(-1, model_width), weights, segments, old_first, old_second
+    attended = attend(q, k, vt, segments)
+    summed, head_far, new_weights = scatter_parts(
+        tables, attended.reshape(16, -1, attended.shape[1]), weights, head_weight
     )
-    summed, heads_used, new_weights = scatter_parts(
-        tables, attended.reshape(16, -1, group_cols), weights, head_weight
+    loss, new_first, new_second = finish(
+        tables, summed, xown, norm_gain[None, :], targets, head_weight, head_far, moments
     )
-    loss = finish(summed, xown, norm_gain[None, :], heads_used, targets)[0]
-    return (new_weights, new_first, new_second, loss)
+    return (new_weights, new_first, new_second, loss[0])
 
 
 def solution(mesh):

time: 316 us -> 284 us (0.90)
  Pallas kernels: 299 us -> 270 us
  local copies, waits for them, and re-layouts: 15 us -> 11.8 us
    pallas_call x2, Pallas kernels: 140 us -> 97.8 us  [the longest x1 78 us: finish(): pl.pallas_call(finish_kernel, name='finish', out_shape=(jax.ShapeDtypeStr...]
    pallas_call x1, Pallas kernels: 95.8 us -> 105 us  [gather_inputs(): pl.pallas_call(gather_kernel, name='gather_inputs', out_shape=(jax.ShapeD...]
    pallas_call x1, Pallas kernels: 63 us -> 66.7 us  [scatter_parts(): pl.pallas_call(scatter_kernel, name='scatter_parts', out_shape=(jax.Shape...]
where the time goes in v4:
time: 284 us
  Pallas kernels  270 us (95%)
  local copies, waits for them, and re-layouts  11.8 us (4%)
    pallas_call x1, Pallas kernels, gather_inputs(): pl.pallas_call(gather_kernel, name='gather_inputs', out_shape=(jax.ShapeD...  105 us
    pallas_call x1, Pallas kernels, finish(): pl.pallas_call(finish_kernel, name='finish', out_shape=(jax.ShapeDtypeStr...  78 us
    pallas_call x1, Pallas kernels, scatter_parts(): pl.pallas_call(scatter_kernel, name='scatter_parts', out_shape=(jax.Shape...  66.7 us
    pallas_call x1, Pallas kernels, attend(): pl.pallas_call(attend_kernel, name='attend', out_shape=jax.ShapeDtypeStru...  19.7 us

profile of v4, /device:TPU:1, one launch (start us, length us, event | category | flops | bytes accessed | tf_op | source)
XLA Modules:
  0.0 284.1 jit_solution(2977425263421508561)
XLA Ops:
  1.9 0.7 broadcast_in_dim.19.mark
  2.6 1.5 stack.8.small
  4.1 105.2 %gather_inputs.1 = (bf16[128,3072]{1,0:T(8,128)(2,1)}, s32[16,8,128]{2,1,0:T(8,128)}, bf16[4,3072,256]{2,1,0:T(8,128)(2,1)}, s32[8,128]{1,0:T(8,128)}, bf16[2048...) custom-call(bf16[128,3072]{1,0:T(8,128)(2,1)} %tok.1, ...), custom_call_target="tpu_custom_call" | custom-call | tf_op jit(solution)/shard_map/gather_inputs/pallas_call | solution.py:562
  109.3 1.5 fusion
  110.8 0.1 copy.22
  110.9 0.2 convert_reduce_fusion
  111.1 0.5 and_select_fusion.begin
  111.7 1.3 copy.20.seg_col
  113.0 19.7 %attend.1 = bf16[2048,256]{1,0:T(8,128)(2,1)} custom-call(s32[8]{0:T(128)} %and_select_fusion.begin, bf16[2048,256]{1,0:T(8,128)(2,1)} %get-tuple-element.20.q, bf16[2048,256]{1,0:T(8,128)(2,1)} %get-tuple-element.21.k, bf16[256,2048]{1,0:T(8,128)(2,1)} %get-tuple-element.22.vt, s32[1,2048]{1,0:T(1,128)} %get-tuple-element.34.seg_row, s32[2048,1]{1,0:T(8,128)} %copy.20.seg_col), custom_call_target="tpu_custom_call" | custom-call | tf_op jit(solution)/shard_map/attend/pallas_call | solution.py:1156
  132.7 66.7 %scatter_parts.1 = (f32[128,3072]{1,0:T(8,128)}, bf16[3072,1024]{1,0:T(8,128)(2,1)}, bf16[4,384,256]{2,1,0:T(8,128)(2,1)}) custom-call(s32[8,128]{1,0:T(8,128)} %get-tuple-element.18.tables, bf16[16,128,256]{2,1,0:T(8,128)(2,1)} %bitcast.17, bf16[4,3072,256]{2,1,0:T(8,128)(2,1)} %get-tuple-element.23.w_all, bf16[3072,1024]{1,0:T(8,128)(2,1)} %hw_own.1), custom_call_target="tpu_custom_call" | custom-call | tf_op jit(solution)/shard_map/scatter_parts/pallas_call | solution.py:807
  199.4 1.3 copy.21.tcol
  200.7 0.0 copy-start.2
  200.7 78.0 %finish.1 = (f32[8,128]{1,0:T(8,128)}, f32[4,384,256]{2,1,0:T(8,128)}, f32[4,384,256]{2,1,0:T(8,128)}) custom-call(s32[8,128]{1,0:T(8,128)} %get-tuple-element.18.tables, f32[128,3072]{1,0:T(8,128)} %get-tuple-element.25.summed, bf16[128,3072]{1,0:T(8,128)(2,1)} %get-tuple-element.26.xown, f32[1,3072]{1,0:T(1,128)} %bitcast.27, s32[16,128,1]{2,1,0:T(8,128)} %copy.21.tcol, ...), custom_call_target="tpu_custom_call" | custom-call | tf_op jit(solution)/shard_map/finish/pallas_call | solution.py:1077
  278.8 0.0 copy-start.1
  278.8 1.3 slice_bitcast_fusion
  280.1 0.0 copy-done.2
  280.1 0.9 copy.28
  281.0 0.0 copy-done.1
  281.0 0.0 copy-start
  281.0 1.1 copy.29
  282.2 0.8 copy-done
  283.0 1.1 copy.30
  (3 shorter events, 0.0 us)
Async XLA Ops:
  200.7 79.4 %copy-start.2 = (bf16[4,384,256]{2,1,0:T(8,128)(2,1)S(1)}, bf16[4,384,256]{2,1,0:T(8,128)(2,1)}, u32[]{:S(2)}) copy-start(bf16[4,384,256]{2,1,0:T(8,128)(2,1)} %get-tuple-element.41) | copy-start | bytes 2359300
  278.8 2.2 copy-start.1
  281.0 2.0 copy-start
